TPU v7x, 512 devices: a whole 4x8x8 slice. The times are simulated.
512 devices in a mesh: tp: 16 (over z, core), ep: 32 (over y, x).
Axes of the slice: x: 4, y: 8, z: 8, core: 2. Of those that a mesh axis runs over, the one named last changes fastest.
Arguments:
- tokens: bfloat16 [12288, 2048], P('ep', 'tp'), may hold values from -6 to 6
- norm_gain: float32 [2048], replicated, may hold values from 0.25 to 1.75
- shared_gate: bfloat16 [2048, 2816], P('ep', 'tp'), may hold values from -0.125 to 0.125
- shared_up: bfloat16 [2048, 2816], P('ep', 'tp'), may hold values from -0.125 to 0.125
- shared_down: bfloat16 [2816, 2048], P('tp', 'ep'), may hold values from -0.21875 to 0.21875
- expert_gate: bfloat16 [16, 32, 176, 2048], P('tp', 'ep'), may hold values from -0.125 to 0.125
- expert_up: bfloat16 [16, 32, 176, 2048], P('tp', 'ep'), may hold values from -0.125 to 0.125
- expert_down: bfloat16 [64, 1408, 2048], P('ep', None, 'tp'), may hold values from -0.15625 to 0.15625
- chosen: int32 [64, 384], P('ep'), may hold values from 0 to 12287, as said below
- gates: float32 [64, 384], P('ep'), may hold values from 0.1 to 1
Outputs:
- mixed: bfloat16 [12288, 2048], P('ep', 'tp')
Inputs may be any that keep to these rules, and one draw needn't show every extreme that they name: Each row of chosen holds 384 different token indices in rising order. Of one row, at most 24 lie among the 384 tokens of one index of ep (tokens s * 384 to (s + 1) * 384 - 1), and in every row exactly 24 lie among those of some index.
All inputs are finite; a program needn't handle non-finite values.
Results may differ from a plain program's by a relative error of at most 0.012.
Values may be sent and summed in bfloat16 or wider, within the bound.
A program may use at most 64 MiB of HBM per device.

v0:
```python
import jax
import jax.numpy as jnp
from jax import lax
from jax.sharding import PartitionSpec as P

EXP_DEV = 2
TOK_DEV = 384
CAP = 384


norm_eps = 1e-06


def side_by_side(arrays, axis, dim, along):
    both = jnp.concatenate(arrays, axis=along)
    whole, at, gathered = (lax.all_gather(both, axis, axis=dim, tiled=True), 0, [])
    for a in arrays:
        gathered.append(lax.slice_in_dim(whole, at, at + a.shape[along], axis=along))
        at += a.shape[along]
    return tuple(gathered)


def sent_to_all(array, axis):
    length = lax.axis_size(axis)
    return lax.all_to_all(
        jnp.broadcast_to(array[None], (length, *array.shape)), axis, 0, 0, tiled=True
    )


def joined_along(pieces, dim):
    dims = list(pieces.shape[1:])
    dims[dim] *= pieces.shape[0]
    return jnp.moveaxis(pieces, 0, dim).reshape(dims)


def gathered_copies(array, axis, dim):
    pieces = sent_to_all(array, axis)
    return joined_along(pieces, dim)


def on_device(
    tokens,
    norm_gain,
    shared_gate,
    shared_up,
    shared_down,
    expert_gate,
    expert_up,
    expert_down,
    chosen,
    gates,
):
    tp_count = lax.axis_size("tp")
    ep_count = lax.axis_size("ep")
    slice_width = tokens.shape[1]
    whole = lax.all_gather(tokens, "tp", axis=1, tiled=True)
    widened = whole.astype(jnp.float32)
    inv_scale = lax.rsqrt(jnp.mean(widened * widened, axis=1, keepdims=True) + norm_eps)
    normed = (widened * inv_scale * norm_gain).astype(jnp.bfloat16)
    pieces = side_by_side((shared_gate, shared_up), "ep", 0, 1)
    gate_sum = jnp.dot(normed, pieces[0], preferred_element_type=jnp.float32)
    up_sum = jnp.dot(normed, pieces[1], preferred_element_type=jnp.float32)
    shared_hidden = (jax.nn.silu(gate_sum) * up_sum).astype(jnp.bfloat16)
    partial_out = jnp.dot(
        shared_hidden, gathered_copies(shared_down, "ep", 1), preferred_element_type=jnp.float32
    )
    shared_part = lax.psum_scatter(
        partial_out.astype(jnp.bfloat16), "tp", scatter_dimension=1, tiled=True
    ).astype(jnp.float32)
    slot_most = 2 * CAP // ep_count
    slot_count = ep_count * slot_most
    sources = chosen // TOK_DEV
    source_flags = (
        sources[:, :, None] == jnp.arange(ep_count, dtype=jnp.int32)[None, None, :]
    ).astype(jnp.int32)
    counts = jnp.sum(source_flags, axis=1)
    starts = jnp.cumsum(counts, axis=1) - counts
    run_start = jnp.take_along_axis(starts, sources, axis=1)
    slot_index = sources * slot_most + jnp.arange(CAP, dtype=jnp.int32)[None, :] - run_start
    local_ids = chosen - sources * TOK_DEV
    expert_rows = jnp.arange(EXP_DEV, dtype=jnp.int32)[:, None]
    requests = (
        jnp.full((EXP_DEV, slot_count), TOK_DEV, jnp.int32)
        .at[expert_rows, slot_index]
        .set(local_ids)
    )
    requests = requests.reshape(EXP_DEV, ep_count, slot_most)
    asked_ids = lax.all_to_all(requests, "ep", split_axis=1, concat_axis=1, tiled=True)
    clipped = jnp.minimum(asked_ids, TOK_DEV - 1)
    local_expert = lax.axis_index("tp") // (tp_count // EXP_DEV)
    own_requests = lax.dynamic_index_in_dim(clipped, local_expert, 0, keepdims=False)
    outgoing = jnp.take(normed, own_requests.reshape(-1), axis=0).reshape(ep_count, slot_most, -1)
    arrived = lax.all_to_all(outgoing, "ep", split_axis=0, concat_axis=0, tiled=True)
    token_rows = arrived.reshape(slot_count, -1)
    gate_weight = expert_gate.reshape(expert_gate.shape[2], expert_gate.shape[3])
    up_weight = expert_up.reshape(expert_up.shape[2], expert_up.shape[3])
    gate_values = jnp.einsum(
        "hd,rd->hr", gate_weight, token_rows, preferred_element_type=jnp.float32
    )
    up_values = jnp.einsum("hd,rd->hr", up_weight, token_rows, preferred_element_type=jnp.float32)
    part_hidden = (jax.nn.silu(gate_values) * up_values).astype(jnp.bfloat16)
    all_hidden = lax.all_gather(part_hidden, "tp", axis=0, tiled=True)
    width_hidden = expert_down.shape[1]
    placed_rows = []
    for expert_slot in range(EXP_DEV):
        hidden_block = all_hidden[expert_slot * width_hidden : (expert_slot + 1) * width_hidden, :]
        outputs = jnp.einsum(
            "fr,fd->rd", hidden_block, expert_down[expert_slot], preferred_element_type=jnp.float32
        )
        gate_slots = (
            jnp.zeros((slot_count,), jnp.float32)
            .at[slot_index[expert_slot]]
            .set(gates[expert_slot])
        )
        placed = (gate_slots[:, None] * outputs).astype(jnp.bfloat16)
        placed_rows.append(placed)
    stacked = jnp.stack(placed_rows).reshape(EXP_DEV, ep_count, slot_most, slice_width)
    returned = lax.all_to_all(stacked, "ep", split_axis=1, concat_axis=1, tiled=True)
    flat_values = returned.reshape(-1, slice_width)
    flat_ids = asked_ids.reshape(-1)
    picker = (jnp.arange(TOK_DEV, dtype=jnp.int32)[:, None] == flat_ids[None, :]).astype(
        jnp.bfloat16
    )
    routed = jnp.dot(picker, flat_values, preferred_element_type=jnp.float32)
    return (shared_part + routed).astype(jnp.bfloat16)


def solution(mesh):
    return jax.shard_map(
        on_device,
        mesh=mesh,
        in_specs=(
            P("ep", "tp"),
            P(),
            P("ep", "tp"),
            P("ep", "tp"),
            P("tp", "ep"),
            P("tp", "ep", None, None),
            P("tp", "ep", None, None),
            P("ep", None, "tp"),
            P("ep", None),
            P("ep", None),
        ),
        out_specs=P("ep", "tp"),
        check_vma=False,
    )
```

profile of v0, /device:TPU:1, one launch (start us, length us, event | category | flops | bytes accessed | tf_op | source)
XLA Modules:
  0.0 283.2 jit_solution(4781293270764742484)
XLA Ops:
  7.4 0.7 all-gather.4.cloned.1.call-update
  8.1 0.7 multiply_subtract_fusion
  9.2 6.6 %gather_fusion.1 = s32[768]{0:T(1024)S(1)} fusion(s32[2,32]{1,0:T(2,128)S(1)} %sub.20, s32[768]{0:T(1024)S(1)} %reshape.168), kind=kCustom, calls=%fused_computation.1 | custom fusion | bytes 12288 | tf_op jit(solution)/shard_map/jit(take_along_axis)/gather | solution.py:78
  15.9 36.5 %scatter_fusion = s32[2,768]{1,0:T(2,128)S(1)} fusion(s32[2,768]{1,0:T(2,128)S(1)} %broadcast_in_dim.23, s32[768]{0:T(1024)S(1)} %reshape.174, s32[768]{0:T(1024)S(1)} %reshape.176), kind=kCustom, calls=%fused_computation.2 | custom fusion | bytes 15360 | tf_op jit(solution)/shard_map/scatter | solution.py:85
  53.1 10.5 %all-to-all-start.1 = ((s32[2,32,24]{2,0,1:T(2,128)}), s32[2,32,24]{2,0,1:T(2,128)S(1)}, u32[]{:S(2)}, u32[]{:S(2)}) async-start(s32[2,32,24]{2,0,1:T(2,128)} %copy.21), calls=%async_computation.1 | async-start | bytes 65536 | tf_op jit(solution)/shard_map/all_to_all | solution.py:88
  63.6 8.7 %all-to-all-done.1 = s32[2,32,24]{2,0,1:T(2,128)S(1)} async-done(((s32[2,32,24]{2,0,1:T(2,128)}), s32[2,32,24]{2,0,1:T(2,128)S(1)}, u32[]{:S(2)}, u32[]{:S(2)}) %all-to-all-start.1) | async-done | bytes 6176 | tf_op jit(solution)/shard_map/all_to_all | solution.py:88
  72.8 0.7 fusion.55
  73.7 1.9 fusion
  76.1 4.3 %gather_fusion = bf16[768,2048]{1,0:T(8,128)(2,1)} fusion(bf16[384,2048]{1,0:T(8,128)(2,1)S(1)} %fusion.2, s32[1024]{0:T(1024)S(1)} %pad_clamp_fusion), kind=kCustom, calls=%fused_computation | custom fusion | bytes 6294528 | tf_op jit(solution)/shard_map/jit(_take)/gather | solution.py:92
  80.3 3.9 %broadcast_select_fusion = bf16[32,24,2048]{2,1,0:T(8,128)(2,1)} fusion(bf16[32,24,2048]{2,1,0:T(8,128)(2,1)} %bitcast.63, pred[32,24]{1,0:T(8,128)(4,1)S(1)} %compare_and_fusion), kind=kLoop, calls=%fused_computation.10 | loop fusion | flops 1572864 | bytes 6292224 | tf_op jit(solution)/shard_map/jit(_take)/select_n | solution.py:92
  84.3 5.0 %all-to-all-start.2 = ((bf16[32,24,2048]{2,1,0:T(8,128)(2,1)}), bf16[32,24,2048]{2,1,0:T(8,128)(2,1)}, u32[]{:S(2)}, u32[]{:S(2)}) async-start(bf16[32,24,2048]{2,1,0:T(8,128)(2,1)} %broadcast_select_fusion), calls=%async_computation.2 | async-start | bytes 6291456 | tf_op jit(solution)/shard_map/all_to_all | solution.py:93
  89.3 0.7 pad_maximum_fusion.1
  90.1 71.4 %all-to-all-done.2 = bf16[32,24,2048]{2,1,0:T(8,128)(2,1)} async-done(((bf16[32,24,2048]{2,1,0:T(8,128)(2,1)}), bf16[32,24,2048]{2,1,0:T(8,128)(2,1)}, u32[]{:S(2)}, u32[]{:S(2)}) %all-to-all-start.2) | async-done | bytes 3145760 | tf_op jit(solution)/shard_map/all_to_all | solution.py:93
  161.5 3.2 %convolution_bitcast_fusion.1 = f32[176,768]{1,0:T(8,128)S(1)} fusion(bf16[768,2048]{1,0:T(8,128)(2,1)} %bitcast.7, bf16[1,1,176,2048]{3,2,1,0:T(8,128)(2,1)S(1)} %copy-done), kind=kOutput, calls=%fused_computation.19 | convolution fusion | flops 553648128 | bytes 4407296 | tf_op jit(solution)/shard_map/hd,rd->hr/dot_general | solution.py:97
  164.6 3.8 %fusion.9 = bf16[176,768]{1,0:T(8,128)(2,1)} fusion(bf16[768,2048]{1,0:T(8,128)(2,1)} %bitcast.7, bf16[1,1,176,2048]{3,2,1,0:T(8,128)(2,1)S(1)} %copy-done.8, f32[176,768]{1,0:T(8,128)S(1)} %convolution_bitcast_fusion.1), kind=kOutput, calls=%fused_computation.21 | convolution fusion | flops 554459136 | bytes 4677632 | tf_op jit(solution)/shard_map/hd,rd->hr/dot_general | solution.py:100
  168.5 1.1 broadcast_in_dim.19
  169.6 6.3 %all-to-all-start = ((bf16[32,176,64]{1,2,0:T(8,128)(2,1)}), bf16[32,176,64]{1,2,0:T(8,128)(2,1)S(1)}, u32[]{:S(2)}, u32[]{:S(2)}) async-start(bf16[32,176,64]{1,2,0:T(8,128)(2,1)} %broadcast_in_dim.19), calls=%async_computation | async-start | bytes 2097152 | tf_op jit(solution)/shard_map/all_to_all | solution.py:25
  175.9 6.8 %all-gather.6.cloned.1.call-done = bf16[2048,352]{1,0:T(8,128)(2,1)} async-done(((bf16[64,352]{1,0:T(8,128)(2,1)}), bf16[2048,352]{1,0:T(8,128)(2,1)}) %all-gather.6.cloned.1.call-update) | async-done | bytes 1441808 | tf_op jit(solution)/shard_map/all_gather | solution.py:16
  182.8 2.6 fusion.28
  185.4 16.2 %all-to-all-done = bf16[32,176,64]{1,2,0:T(8,128)(2,1)S(1)} async-done(((bf16[32,176,64]{1,2,0:T(8,128)(2,1)}), bf16[32,176,64]{1,2,0:T(8,128)(2,1)S(1)}, u32[]{:S(2)}, u32[]{:S(2)}) %all-to-all-start) | async-done | bytes 720928 | tf_op jit(solution)/shard_map/all_to_all | solution.py:25
  201.6 4.3 %convolution_convert_fusion = bf16[384,2048]{1,0:T(8,128)(2,1)} fusion(bf16[176,2048]{0,1:T(8,128)(2,1)S(1)} %bitcast.65, bf16[384,2048]{1,0:T(8,128)(2,1)S(1)} %fusion.2, bf16[2048,352]{1,0:T(8,128)(2,1)} %all-gather.6.cloned.1.call-done, f32[384,176]{0,1:T(8,128)} %fusion.28), kind=kOutput, calls=%fused_computation.11 | convolution fusion | flops 554840064 | bytes 5185536 | tf_op jit(solution)/shard_map/dot_general | solution.py:64
  205.9 2.7 copy.26
  208.7 3.1 %scatter_custom_fusion.1 = f32[768]{0:T(1024)S(1)} fusion(s32[384]{0:T(512)S(1)} %get-tuple-element.7, f32[384]{0:T(512)S(1)} %get-tuple-element.5, f32[]{:T(128)} %constant.48.clone.1), kind=kCustom, calls=%fused_computation.73 | custom fusion | bytes 3076 | tf_op jit(solution)/shard_map/scatter | solution.py:113
  211.8 2.9 %scatter_custom_fusion.2 = f32[768]{0:T(1024)S(1)} fusion(s32[384]{0:T(512)S(1)} %get-tuple-element.8, f32[384]{0:T(512)S(1)} %get-tuple-element.6, f32[]{:T(128)} %constant.48.clone.1), kind=kCustom, calls=%fused_computation.71 | custom fusion | bytes 3076 | tf_op jit(solution)/shard_map/scatter | solution.py:113
  214.7 20.1 %all-gather.8.cloned.1.call-done = bf16[2816,768]{1,0:T(8,128)(2,1)} async-done(((bf16[176,768]{1,0:T(8,128)(2,1)}), bf16[2816,768]{1,0:T(8,128)(2,1)}) %all-gather.8.cloned.1.call-update) | async-done | bytes 4325392 | tf_op jit(solution)/shard_map/all_gather | solution.py:102
  234.8 2.5 fusion.17
  237.7 0.8 fusion.20
  238.5 0.8 pad_maximum_fusion
  239.2 9.5 %all-to-all-start.3 = ((bf16[2,32,24,128]{3,2,0,1:T(8,128)(2,1)}), bf16[2,32,24,128]{3,2,0,1:T(8,128)(2,1)S(1)}, u32[]{:S(2)}, u32[]{:S(2)}) async-start(bf16[2,32,24,128]{3,2,0,1:T(8,128)(2,1)} %pad_maximum_fusion), calls=%async_computation.3 | async-start | bytes 786432 | tf_op jit(solution)/shard_map/all_to_all | solution.py:118
  248.9 24.6 %reduce-scatter.4.cloned.1.call-done = bf16[128,384]{1,0:T(8,128)(2,1)} async-done(((bf16[2048,384]{1,0:T(8,128)(2,1)}), bf16[128,384]{1,0:T(8,128)(2,1)}) %reduce-scatter.4.cloned.1.call-update) | async-done | bytes 98320
  273.5 1.0 copy.27
  274.6 1.2 fusion.25
  (53 shorter events, 3.0 us)
Async XLA Ops:
  7.4 154.1 %copy-start = (bf16[1,1,176,2048]{3,2,1,0:T(8,128)(2,1)S(1)}, bf16[1,1,176,2048]{3,2,1,0:T(8,128)(2,1)}, u32[]{:S(2)}) copy-start(bf16[1,1,176,2048]{3,2,1,0:T(8,128)(2,1)} %param.15) | copy-start | bytes 2162692
  7.4 66.3 %all-gather.4.cloned.1.call-start = ((), (), s32[]{:S(2)}) async-start(), calls=%async_computation.5 | async-start | bytes 1671168 | tf_op jit(solution)/shard_map/all_gather | solution.py:56
  15.8 59.8 %copy-start.5 = (f32[2048]{0:T(1024)S(1)}, f32[2048]{0:T(1024)}, u32[]{:S(2)}) copy-start(f32[2048]{0:T(1024)} %param.11) | copy-start | bytes 24580
  53.1 19.2 %all-to-all-start.1 = ((s32[2,32,24]{2,0,1:T(2,128)}), s32[2,32,24]{2,0,1:T(2,128)S(1)}, u32[]{:S(2)}, u32[]{:S(2)}) async-start(s32[2,32,24]{2,0,1:T(2,128)} %copy.21), calls=%async_computation.1 | async-start | bytes 65536 | tf_op jit(solution)/shard_map/all_to_all | solution.py:88
  73.7 1.9 copy-start.1
  84.3 5.0 %copy-start.2 = (bf16[64,176]{1,0:T(8,128)(2,1)S(1)}, bf16[64,176]{1,0:T(8,128)(2,1)}, u32[]{:S(2)}) copy-start(bf16[64,176]{1,0:T(8,128)(2,1)} %param.13) | copy-start | bytes 67588
  84.3 5.0 %copy-start.3 = (bf16[64,176]{1,0:T(8,128)(2,1)S(1)}, bf16[64,176]{1,0:T(8,128)(2,1)}, u32[]{:S(2)}) copy-start(bf16[64,176]{1,0:T(8,128)(2,1)} %param.12) | copy-start | bytes 67588
  84.3 77.2 %all-to-all-start.2 = ((bf16[32,24,2048]{2,1,0:T(8,128)(2,1)}), bf16[32,24,2048]{2,1,0:T(8,128)(2,1)}, u32[]{:S(2)}, u32[]{:S(2)}) async-start(bf16[32,24,2048]{2,1,0:T(8,128)(2,1)} %broadcast_select_fusion), calls=%async_computation.2 | async-start | bytes 6291456 | tf_op jit(solution)/shard_map/all_to_all | solution.py:93
  89.2 93.6 %all-gather.6.cloned.1.call-start = ((), (), s32[]{:S(2)}) async-start(), calls=%async_computation.6 | async-start | bytes 1622016 | tf_op jit(solution)/shard_map/all_gather | solution.py:16
  90.0 144.7 %all-gather.8.cloned.1.call-start = ((), (), s32[]{:S(2)}) async-start(), calls=%async_computation.7 | async-start | bytes 4595712 | tf_op jit(solution)/shard_map/all_gather | solution.py:102
  161.5 3.2 %copy-start.8 = (bf16[1,1,176,2048]{3,2,1,0:T(8,128)(2,1)S(1)}, bf16[1,1,176,2048]{3,2,1,0:T(8,128)(2,1)}, u32[]{:S(2)}) copy-start(bf16[1,1,176,2048]{3,2,1,0:T(8,128)(2,1)} %param.16) | copy-start | bytes 2162692
  164.6 3.9 %copy-start.4 = (bf16[176,64]{0,1:T(8,128)(2,1)S(1)}, bf16[176,64]{0,1:T(8,128)(2,1)}, u32[]{:S(2)}) copy-start(bf16[176,64]{0,1:T(8,128)(2,1)} %param.14) | copy-start | bytes 67588
  169.6 32.0 %all-to-all-start = ((bf16[32,176,64]{1,2,0:T(8,128)(2,1)}), bf16[32,176,64]{1,2,0:T(8,128)(2,1)S(1)}, u32[]{:S(2)}, u32[]{:S(2)}) async-start(bf16[32,176,64]{1,2,0:T(8,128)(2,1)} %broadcast_in_dim.19), calls=%async_computation | async-start | bytes 2097152 | tf_op jit(solution)/shard_map/all_to_all | solution.py:25
  175.9 97.6 %reduce-scatter.4.cloned.1.call-start = ((), (), s32[]{:S(2)}) async-start(), calls=%async_computation.8 | async-start | bytes 1671168
  205.9 2.7 copy-start.6
  205.9 28.9 %copy-start.9 = (bf16[2,1408,128]{2,1,0:T(8,128)(2,1)S(1)}, bf16[2,1408,128]{2,1,0:T(8,128)(2,1)}, u32[]{:S(2)}) copy-start(bf16[2,1408,128]{2,1,0:T(8,128)(2,1)} %param.17) | copy-start | bytes 2162692
  234.8 2.9 %copy-start.7 = (bf16[2816,768]{1,0:T(8,128)(2,1)S(1)}, bf16[2816,768]{1,0:T(8,128)(2,1)}, u32[]{:S(2)}) copy-start(bf16[2816,768]{1,0:T(8,128)(2,1)} %all-gather.8.cloned.1.call-done) | copy-start | bytes 12976132
  239.2 35.2 %all-to-all-start.3 = ((bf16[2,32,24,128]{3,2,0,1:T(8,128)(2,1)}), bf16[2,32,24,128]{3,2,0,1:T(8,128)(2,1)S(1)}, u32[]{:S(2)}, u32[]{:S(2)}) async-start(bf16[2,32,24,128]{3,2,0,1:T(8,128)(2,1)} %pad_maximum_fusion), calls=%async_computation.3 | async-start | bytes 786432 | tf_op jit(solution)/shard_map/all_to_all | solution.py:118
Sparse Core Ops, SparseCore 0:
  10.2 48.0 all-gather.3
  208.7 64.7 reduce-scatter.3
Sparse Core Ops, SparseCore 1:
  92.9 89.9 all-gather.5
  184.8 49.9 all-gather.7
where the time goes:
time: 286 us; the launch traced here: 283 us
  waiting for transfers between devices  149 us (52%)
  local copies, waits for them, and re-layouts  60.1 us (21%)
  starting transfers between devices  31.4 us (11%)
  matrix products  18.4 us (6%)
  between operations  15.2 us (5%)
  other arithmetic  9.57 us (3%)
    all_to_all x1, waiting for transfers between devices, on_device(): lax.all_to_all(outgoing, 'ep', split_axis=0, concat_axis=0, tiled=True)  71.4 us
    scatter x1, local copies, waits for them, and re-layouts, on_device(): requests = jnp.full((EXP_DEV, slot_count), TOK_DEV, jnp.int32).at[expert_...  36.5 us
    unnamed x5, waiting for transfers between devices  25.4 us
    all_gather x1, waiting for transfers between devices, on_device(): all_hidden = lax.all_gather(part_hidden, 'tp', axis=0, tiled=True)  20.1 us
    all_to_all x1, waiting for transfers between devices, sent_to_all(): lax.all_to_all(jnp.broadcast_to(array[None], (length, *array.shape)), axi...  16.2 us
    all_to_all x1, starting transfers between devices, on_device(): lax.all_to_all(requests, 'ep', split_axis=1, concat_axis=1, tiled=True)  10.5 us
    all_to_all x1, starting transfers between devices, on_device(): lax.all_to_all(stacked, 'ep', split_axis=1, concat_axis=1, tiled=True)  9.52 us
    all_to_all x1, waiting for transfers between devices, on_device(): lax.all_to_all(requests, 'ep', split_axis=1, concat_axis=1, tiled=True)  8.68 us
  transfers between devices with their start and end apart: 8, of which 6 were waited for; matrix products, arithmetic and copies ran while one was open for 27% of the time, Pallas kernels for 0%

commit v1 on v0

v1 whole, which is shorter than its diff:
```python
import functools

import jax
import jax.numpy as jnp
from jax import lax
from jax.experimental import pallas as pl
from jax.experimental.pallas import tpu as pltpu
from jax.sharding import PartitionSpec as P

MESH = pl.DeviceIdType.MESH
EXP_DEV = 2
TOK_DEV = 384
CAP = 384
NZ, NY, NX = 8, 8, 4
N_TP, N_EP = 16, 32
SLOT = 24
PER = EXP_DEV * SLOT
SLOTS = N_EP * PER
F_DEV = 176
D = 2048
W = 128
norm_eps = 1e-06
bf16 = jnp.bfloat16
f32 = jnp.float32


class Link:
    def __init__(self, send_sems, recv_sems):
        self.send_sems, self.recv_sems = send_sems, recv_sems
        self.keys, self.sent = {}, []

    def _at(self, key):
        return self.keys.setdefault(key, len(self.keys))

    def _copy(self, src, dst, key, device):
        i = self._at(key)
        return pltpu.make_async_remote_copy(
            src_ref=src,
            dst_ref=dst,
            send_sem=self.send_sems.at[i],
            recv_sem=self.recv_sems.at[i],
            device_id=device,
            device_id_type=MESH,
        )

    def send(self, src, dst, key, device):
        copy = self._copy(src, dst, key, device)
        copy.start()
        self.sent.append(copy)

    def arrive(self, dst, key, device):
        self._copy(dst, dst, key, device).wait_recv()

    def finish(self):
        for copy in self.sent:
            copy.wait_send()


def places():
    tp, ep = lax.axis_index("tp"), lax.axis_index("ep")
    return tp // 2, lax.rem(tp, 2), ep // NX, lax.rem(ep, NX)


def around(position, step, count):
    return lax.rem(position + step + count, count)


def z_device(z, core):
    return {"tp": z * 2 + core}


def greet(z_ring, plane, lines):
    barrier = pltpu.get_barrier_semaphore()
    z, core, y, x = places()
    devices = []
    if z_ring:
        devices += [z_device(around(z, 1, NZ), core), z_device(around(z, -1, NZ), core)]
        devices += [z_device(z, 1 - core)]
    if plane:
        devices += [{"ep": around(y, a, NY) * NX + around(x, b, NX)} for a, b in OFFSETS]
    if lines:
        devices += [{"ep": around(y, a, NY) * NX + x} for a in (1, -1)]
        devices += [{"ep": y * NX + around(x, b, NX)} for b in (1, -1)]
    for device in devices:
        pl.semaphore_signal(barrier, inc=1, device_id=device, device_id_type=MESH)
    return len(devices)


def met(count):
    pl.semaphore_wait(pltpu.get_barrier_semaphore(), count)


OFFSETS = sorted(
    [(a, b) for a in range(-3, 5) for b in range(-1, 3) if (a, b) != (0, 0)],
    key=lambda o: (-abs(o[0]) - abs(o[1]), o),
)


def exchange_start(src, dst, send_sem, recv_sem):
    _, _, y, x = places()
    own = y * NX + x
    for a, b in OFFSETS:
        peer = around(y, a, NY) * NX + around(x, b, NX)
        pltpu.make_async_remote_copy(
            src_ref=src.at[peer],
            dst_ref=dst.at[own],
            send_sem=send_sem,
            recv_sem=recv_sem,
            device_id={"ep": peer},
            device_id_type=MESH,
        ).start()
    dst[own] = src[own]


def exchange_wait(src, dst, send_sem, recv_sem):
    part = pl.ds(0, N_EP - 1)
    pltpu.make_async_copy(dst.at[part], dst.at[part], recv_sem).wait()
    pltpu.make_async_copy(src.at[part], src.at[part], send_sem).wait()


def reach(direction, flipped):
    return 4 if (direction > 0) != bool(flipped) else 3


def ring_gather(src, dst, link, cuts):
    z, core, _, _ = places()
    own = z * 2 + core
    other = z_device(z, 1 - core)
    beside = {d: z_device(around(z, d, NZ), core) for d in (1, -1)}
    for h, rows in enumerate(cuts):
        for d in (1, -1):
            link.send(src.at[rows], dst.at[own, rows], (d, 1, h), beside[d])
    for h, rows in enumerate(cuts):
        link.send(src.at[rows], dst.at[own, rows], ("core", 0, 0, h), other)
    dst[own] = src[...]
    yield
    for k in range(1, 5):
        for h, rows in enumerate(cuts):
            for d in (1, -1):
                most = reach(d, h % 2)
                if k > most:
                    continue
                block = dst.at[around(z, -d * k, NZ) * 2 + core, rows]
                link.arrive(block, (d, k, h), other)
                if k < most:
                    link.send(block, block, (d, k + 1, h), beside[d])
                link.send(block, block, ("core", d, k, h), other)
                yield
    for h, rows in enumerate(cuts):
        link.arrive(dst.at[z * 2 + 1 - core, rows], ("core", 0, 0, h), other)
    for k in range(1, 5):
        for h, rows in enumerate(cuts):
            for d in (1, -1):
                if k <= reach(d, h % 2):
                    block = dst.at[around(z, -d * k, NZ) * 2 + 1 - core, rows]
                    link.arrive(block, ("core", d, k, h), other)
                    yield
    link.finish()


def plane_gather(src, dst, link, y_first):
    _, _, y, x = places()
    a, na, b, nb = (y, NY, x, NX) if y_first else (x, NX, y, NY)

    def index(p, q):
        return p * NX + q if y_first else q * NX + p

    own = index(a, b)
    here = {"ep": own}
    along = {d: {"ep": index(around(a, d, na), b)} for d in (1, -1)}
    across = {d: {"ep": index(a, around(b, d, nb))} for d in (1, -1)}
    for d in (1, -1):
        link.send(src, dst.at[own], ("a", d, 1), along[d])
    for d in (1, -1):
        link.send(src, dst.at[own], ("b", d, 1, 0, 0), across[d])
    dst[own] = src[...]
    yield
    tags = [(0, 0)]
    for k in range(1, na // 2 + 1):
        for d in (1, -1):
            most = na // 2 if d > 0 else na // 2 - 1
            if k > most:
                continue
            tags.append((d, k))
            block = dst.at[index(around(a, -d * k, na), b)]
            link.arrive(block, ("a", d, k), here)
            if k < most:
                link.send(block, block, ("a", d, k + 1), along[d])
            for s in (1, -1):
                link.send(block, block, ("b", s, 1, d, k), across[s])
            yield
    for j in range(1, nb // 2 + 1):
        for n, (d, k) in enumerate(tags):
            for s in (1, -1):
                most = nb // 2 if (s > 0) == (n % 2 == 0) else nb // 2 - 1
                if j > most:
                    continue
                block = dst.at[index(around(a, -d * k, na), around(b, -s * j, nb))]
                link.arrive(block, ("b", s, j, d, k), here)
                if j < most:
                    link.send(block, block, ("b", s, j + 1, d, k), across[s])
                yield
    link.finish()


def in_turn(*jobs):
    jobs = list(jobs)
    while jobs:
        for job in list(jobs):
            try:
                next(job)
            except StopIteration:
                jobs.remove(job)


def one_hot(condition):
    return jnp.where(condition, 1.0, 0.0).astype(bf16)


def ask_kernel(req_ref, asked_ref, send_sem, recv_sem):
    met(greet(False, True, False))
    exchange_start(req_ref, asked_ref, send_sem, recv_sem)
    exchange_wait(req_ref, asked_ref, send_sem, recv_sem)


def dispatch_kernel(ids_ref, tok_ref, came_ref, all_ref, out, send_sem, recv_sem, ss, rs):
    count = greet(True, True, False)
    token = lax.broadcasted_iota(jnp.int32, (SLOTS, TOK_DEV), 1)
    picked = jnp.dot(one_hot(token == ids_ref[...]), tok_ref[...], preferred_element_type=f32)
    out[...] = picked.astype(bf16).reshape(N_EP, PER, W)
    met(count)
    exchange_start(out, came_ref, send_sem, recv_sem)
    half = TOK_DEV // 2
    in_turn(ring_gather(tok_ref, all_ref, Link(ss, rs), [pl.ds(0, half), pl.ds(half, half)]))
    exchange_wait(out, came_ref, send_sem, recv_sem)


def join_kernel(slot_ref, came_ref, gu_ref, dn_ref, rows_ref, wg_ref, wd_ref, own, ss, rs, sg, rg, sd, rd):
    count = greet(True, False, True)
    slot = lax.broadcasted_iota(jnp.int32, (EXP_DEV * CAP, SLOTS), 1)
    came = came_ref[...].reshape(SLOTS, W)
    own[...] = jnp.dot(
        one_hot(slot == slot_ref[...]), came, preferred_element_type=f32
    ).astype(bf16)
    met(count)
    in_turn(
        ring_gather(own, rows_ref, Link(ss, rs), [pl.ds(0, CAP), pl.ds(CAP, CAP)]),
        plane_gather(gu_ref, wg_ref, Link(sg, rg), True),
        plane_gather(dn_ref, wd_ref, Link(sd, rd), False),
    )


def hidden_kernel(own_ref, all_ref, ss, rs):
    met(greet(True, False, False))
    in_turn(ring_gather(own_ref, all_ref, Link(ss, rs), [pl.ds(0, 96), pl.ds(96, 80)]))


def back_kernel(
    slot_ref, ids_ref, rows_ref, part_ref, mixed_ref, out, came, pair, got, made, send_sem, recv_sem, ss, rs
):
    count = greet(True, True, False)
    z, core, _, _ = places()
    other = z_device(z, 1 - core)
    slot = lax.broadcasted_iota(jnp.int32, (SLOTS, EXP_DEV * CAP), 0)
    spread = jnp.dot(one_hot(slot == slot_ref[...]), rows_ref[...], preferred_element_type=f32)
    out[...] = spread.astype(bf16).reshape(N_EP, PER, W)
    met(count)
    link = Link(ss, rs)
    order = [4, -4 + 1, 3, -2, 2, -1, 1, 0]
    targets = {m % NZ: around(z, m, NZ) for m in order}
    for m in order:
        at = targets[m % NZ]
        link.send(part_ref.at[at * 2 + 1 - core], pair.at[at], ("core", m % NZ), other)
    exchange_start(out, came, send_sem, recv_sem)
    half = TOK_DEV // 2
    here = set()

    def term(m, rows):
        m = m % NZ
        at = targets[m]
        if m not in here:
            link.arrive(pair.at[at], ("core", m), other)
            here.add(m)
        return part_ref[at * 2 + core, rows].astype(f32) + pair[at, rows].astype(f32)

    cuts = [pl.ds(0, half), pl.ds(half, half)]
    way = {1: 0, -1: 1}
    for k in range(1, 5):
        for h, rows in enumerate(cuts):
            for d in (1, -1):
                most = reach(d, h)
                if k > most:
                    continue
                total = term(d * (most + 1 - k), rows)
                if k > 1:
                    link.arrive(got.at[way[d], k - 1, rows], (d, k - 1, h), other)
                    total = total + got[way[d], k - 1, rows].astype(f32)
                made[way[d], k, rows] = total.astype(bf16)
                link.send(
                    made.at[way[d], k, rows],
                    got.at[way[d], k, rows],
                    (d, k, h),
                    z_device(around(z, d, NZ), core),
                )
    exchange_wait(out, came, send_sem, recv_sem)
    token = lax.broadcasted_iota(jnp.int32, (TOK_DEV, SLOTS), 0)
    routed = jnp.dot(
        one_hot(token == ids_ref[...]), came[...].reshape(SLOTS, W), preferred_element_type=f32
    )
    for h, rows in enumerate(cuts):
        total = term(0, rows)
        for d in (1, -1):
            most = reach(d, h)
            link.arrive(got.at[way[d], most, rows], (d, most, h), other)
            total = total + got[way[d], most, rows].astype(f32)
        mixed_ref[rows, :] = (total + routed[h * half : (h + 1) * half]).astype(bf16)
    link.finish()


def call(kernel, name, ident, operands, outs, scratch):
    vmem = pl.BlockSpec(memory_space=pltpu.VMEM)
    return pl.pallas_call(
        kernel,
        name=name,
        out_shape=[jax.ShapeDtypeStruct(s, d) for s, d in outs],
        in_specs=[vmem] * len(operands),
        out_specs=[vmem] * len(outs),
        scratch_shapes=scratch,
        compiler_params=pltpu.CompilerParams(
            collective_id=ident, has_side_effects=True, vmem_limit_bytes=48 * 1024 * 1024
        ),
    )(*operands)


def sems(n):
    return [pltpu.SemaphoreType.DMA((n,)), pltpu.SemaphoreType.DMA((n,))]


def pair_sems():
    return [pltpu.SemaphoreType.DMA, pltpu.SemaphoreType.DMA]


def scaled(rows, gain):
    wide = jnp.moveaxis(rows, 0, 1).reshape(rows.shape[1], D).astype(f32)
    inv = lax.rsqrt(jnp.mean(wide * wide, axis=1, keepdims=True) + norm_eps)
    return (wide * inv * gain).astype(bf16)


def on_device(
    tokens,
    norm_gain,
    shared_gate,
    shared_up,
    shared_down,
    expert_gate,
    expert_up,
    expert_down,
    chosen,
    gates,
):
    sources = chosen // TOK_DEV
    before = jnp.sum((sources[:, None, :] < sources[:, :, None]).astype(jnp.int32), axis=2)
    rank = jnp.arange(CAP, dtype=jnp.int32)[None, :] - before
    base = jnp.arange(EXP_DEV, dtype=jnp.int32)[:, None] * SLOT
    slots = sources * PER + base + rank
    local_ids = chosen - sources * TOK_DEV
    place = (
        jnp.arange(N_EP, dtype=jnp.int32)[None, :, None] * PER
        + base[:, :, None]
        + jnp.arange(SLOT, dtype=jnp.int32)[None, None, :]
    )
    requests = jnp.max(
        jnp.where(place[:, :, :, None] == slots[:, None, None, :], local_ids[:, None, None, :], -1),
        axis=3,
    )
    requests = jnp.moveaxis(requests, 0, 1).reshape(N_EP, 1, PER)
    requests = jnp.pad(requests, ((0, 0), (0, 0), (0, W - PER)), constant_values=-1)
    (asked,) = call(
        ask_kernel, "ask", 0, [requests], [((N_EP, 1, W), jnp.int32)], pair_sems()
    )
    asked = asked[:, 0, :PER].reshape(SLOTS)

    came, all_tokens = call(
        dispatch_kernel,
        "dispatch",
        1,
        [asked.reshape(SLOTS, 1), tokens],
        [((N_EP, PER, W), bf16), ((N_TP, TOK_DEV, W), bf16)],
        [pltpu.VMEM((N_EP, PER, W), bf16), *pair_sems(), *sems(32)],
    )

    edge = lambda a: a[:, W:]
    gu = jnp.concatenate(
        [
            shared_gate[:, :W],
            shared_up[:, :W],
            edge(shared_gate),
            edge(shared_up),
            jnp.zeros((64, 32), bf16),
        ],
        axis=1,
    )
    dn = jnp.pad(shared_down.T, ((0, 0), (0, 80)))
    rows, wg, wd = call(
        join_kernel,
        "join",
        2,
        [slots.reshape(EXP_DEV * CAP, 1), came, gu, dn],
        [((N_TP, EXP_DEV * CAP, W), bf16), ((N_EP, 64, 384), bf16), ((N_EP, 64, 256), bf16)],
        [pltpu.VMEM((EXP_DEV * CAP, W), bf16), *sems(32), *sems(32), *sems(32)],
    )

    expert = lax.axis_index("tp") // (N_TP // EXP_DEV)
    own_rows = lax.dynamic_slice_in_dim(rows, expert * CAP, CAP, axis=1)
    token_rows = scaled(own_rows, norm_gain)
    gate_weight = expert_gate.reshape(F_DEV, D)
    up_weight = expert_up.reshape(F_DEV, D)
    gate_values = jnp.einsum("hd,rd->hr", gate_weight, token_rows, preferred_element_type=f32)
    up_values = jnp.einsum("hd,rd->hr", up_weight, token_rows, preferred_element_type=f32)
    part_hidden = (jax.nn.silu(gate_values) * up_values).astype(bf16)

    (all_hidden,) = call(
        hidden_kernel, "hidden", 3, [part_hidden], [((N_TP, F_DEV, CAP), bf16)], sems(32)
    )
    all_hidden = all_hidden.reshape(EXP_DEV, N_TP // EXP_DEV * F_DEV, CAP)
    outputs = jnp.einsum("efr,efd->erd", all_hidden, expert_down, preferred_element_type=f32)
    weighted = (gates[:, :, None] * outputs).astype(bf16).reshape(EXP_DEV * CAP, W)

    normed = scaled(all_tokens, norm_gain)
    sums = jnp.dot(normed, wg.reshape(D, 384), preferred_element_type=f32)
    low = jax.nn.silu(sums[:, :W]) * sums[:, W : 2 * W]
    high = jax.nn.silu(sums[:, 256:304]) * sums[:, 304:352]
    shared_hidden = jnp.concatenate([low, high, jnp.zeros((TOK_DEV, 80), f32)], axis=1).astype(bf16)
    blocks = jnp.einsum(
        "rh,tdh->trd", shared_hidden, wd.reshape(N_TP, W, 256), preferred_element_type=f32
    ).astype(bf16)

    (mixed,) = call(
        back_kernel,
        "back",
        4,
        [slots.reshape(1, EXP_DEV * CAP), asked.reshape(1, SLOTS), weighted, blocks],
        [((TOK_DEV, W), bf16)],
        [
            pltpu.VMEM((N_EP, PER, W), bf16),
            pltpu.VMEM((N_EP, PER, W), bf16),
            pltpu.VMEM((NZ, TOK_DEV, W), bf16),
            pltpu.VMEM((2, 5, TOK_DEV, W), bf16),
            pltpu.VMEM((2, 5, TOK_DEV, W), bf16),
            *pair_sems(),
            *sems(32),
        ],
    )
    return mixed


def solution(mesh):
    return jax.shard_map(
        on_device,
        mesh=mesh,
        in_specs=(
            P("ep", "tp"),
            P(),
            P("ep", "tp"),
            P("ep", "tp"),
            P("tp", "ep"),
            P("tp", "ep", None, None),
            P("tp", "ep", None, None),
            P("ep", None, "tp"),
            P("ep", None),
            P("ep", None),
        ),
        out_specs=P("ep", "tp"),
        check_vma=False,
    )
```

time: 286 us -> 146 us (0.51)
  waiting for transfers between devices: 149 us -> 0 us
  Pallas kernels: 0 us -> 120 us
  local copies, waits for them, and re-layouts: 60.1 us -> 10.1 us
  starting transfers between devices: 31.4 us -> 0 us
  between operations: 15.2 us -> 0.3 us
  matrix products: 18.4 us -> 5.34 us
    pallas_call x0 -> x5, Pallas kernels: none -> 120 us  [call(): pl.pallas_call(kernel, name=name, out_shape=[jax.ShapeDtypeStruct(s, d) f...]
    all_to_all x4 -> x0, waiting for transfers between devices: 96.3 us -> none  [the longest x1 71.4 us: on_device(): lax.all_to_all(outgoing, 'ep', split_axis=0, concat_axis=0, tiled=True)]
    scatter x3 -> x0, local copies, waits for them, and re-layouts: 42.5 us -> none  [the longest x1 36.5 us: on_device(): requests = jnp.full((EXP_DEV, slot_count), TOK_DEV, jnp.int32).at[expert_...]
    all_to_all x4 -> x0, starting transfers between devices: 31.2 us -> none  [the longest x1 10.5 us: on_device(): lax.all_to_all(requests, 'ep', split_axis=1, concat_axis=1, tiled=True)]
    all_gather x3 -> x0, waiting for transfers between devices: 26.9 us -> none  [the longest x1 20.1 us: on_device(): all_hidden = lax.all_gather(part_hidden, 'tp', axis=0, tiled=True)]
    unnamed x5 -> x0, waiting for transfers between devices: 25.4 us -> none
    dot_general x7 -> x5, matrix products: 18.4 us -> 5.34 us  [the longest x1 2.53 us: on_device(): sums = jnp.dot(normed, wg.reshape(D, 384), preferred_element_type=f32)]
    gather x4 -> x0, local copies, waits for them, and re-layouts: 10.9 us -> none  [the longest x3 6.63 us: on_device(): run_start = jnp.take_along_axis(starts, sources, axis=1)]
  transfers between devices with their start and end apart: 8 -> 0, of which waited for: 6 -> 0; matrix products, arithmetic and copies ran while one was open for 27% -> 0% of each run, Pallas kernels for 0% -> 0%
where the time goes in v1:
time: 146 us; the launch traced here: 145 us
  Pallas kernels  120 us (82%)
  local copies, waits for them, and re-layouts  10.1 us (7%)
  other arithmetic  9.13 us (6%)
  matrix products  5.34 us (4%)
    pallas_call x5, Pallas kernels, call(): pl.pallas_call(kernel, name=name, out_shape=[jax.ShapeDtypeStruct(s, d) f...  120 us
    convert_element_type x2, local copies, waits for them, and re-layouts, scaled(): return (wide * inv * gain).astype(bf16)  4.68 us
    unnamed x25, local copies, waits for them, and re-layouts  4.54 us
    convert_element_type x1, other arithmetic, scaled(): return (wide * inv * gain).astype(bf16)  4.17 us

profile of v1, /device:TPU:1, one launch (start us, length us, event | category | flops | bytes accessed | tf_op | source)
XLA Modules:
  0.0 144.8 jit_solution(3011367912106522060)
XLA Ops:
  0.0 0.8 multiply_subtract_fusion
  0.8 0.3 convert_reduce_fusion
  1.1 0.1 subtract_add_fusion
  1.2 0.1 broadcast_add_fusion
  1.2 0.1 iota_add_fusion
  1.3 1.4 select_reduce_fusion
  2.7 0.1 copy.22
  2.9 11.8 %ask.1 = s32[32,1,128]{2,1,0:T(1,128)S(1)} custom-call(s32[32,1,128]{2,1,0:T(1,128)S(1)} %pad.8.req_ref), custom_call_target="tpu_custom_call" | custom-call | tf_op jit(solution)/shard_map/ask/pallas_call | solution.py:322
  14.8 0.1 reshape_reshape_squeeze.6.ids_ref
  14.9 0.4 reshape_reshape_squeeze.8.ids_ref
  15.3 0.9 copy-done.3
  16.2 31.8 %dispatch.1 = (bf16[32,48,128]{2,1,0:T(8,128)(2,1)S(1)}, bf16[16,384,128]{2,1,0:T(8,128)(2,1)S(1)}) custom-call(s32[1536,1]{1,0:T(8,128)S(1)} %reshape_reshape_squeeze.8.ids_ref, bf16[384,128]{1,0:T(8,128)(2,1)S(1)} %copy-done.3), custom_call_target="tpu_custom_call" | custom-call | tf_op jit(solution)/shard_map/dispatch/pallas_call | solution.py:322
  48.0 0.4 fusion.3
  48.4 0.2 copy.37
  48.6 0.1 concatenate.7.gu_ref
  48.8 31.6 %join.1 = (bf16[16,768,128]{2,1,0:T(8,128)(2,1)}, bf16[32,64,384]{2,1,0:T(8,128)(2,1)S(1)}, bf16[32,64,256]{2,1,0:T(8,128)(2,1)S(1)}) custom-call(s32[768,1]{1,0:T(8,128)S(1)} %bitcast.49, bf16[32,48,128]{2,1,0:T(8,128)(2,1)S(1)} %get-tuple-element.10.came_ref, bf16[64,384]{1,0:T(8,128)(2,1)S(1)} %concatenate.7.gu_ref, bf16[64,256]{1,0:T(8,128)(2,1)S(1)} %pad.9.dn_ref), custom_call_target="tpu_custom_call" | custom-call | tf_op jit(solution)/shard_map/join/pallas_call | solution.py:322
  80.4 1.1 copy-done.1
  81.5 1.2 copy-done.4
  82.6 1.8 %fusion = f32[384]{0:T(512)S(1)} fusion(bf16[16,768,128]{2,1,0:T(8,128)(2,1)} %get-tuple-element.11, s32[]{:T(128)S(6)} %select_n.20), kind=kLoop, calls=%fused_computation.4 | loop fusion | flops 2358912 | bytes 1574404 | tf_op jit(solution)/shard_map/reduce_sum | solution.py:345
  84.4 4.2 %fusion.6 = (bf16[384,16,128]{2,0,1:T(8,128)(2,1)}, bf16[384,16,128]{2,0,1:T(8,128)(2,1)}) fusion(bf16[16,384,128]{2,1,0:T(8,128)(2,1)S(1)} %get-tuple-element.13, f32[384]{0:T(512)S(1)} %get-tuple-element.21, f32[16,128]{1,0:T(8,128)S(1)} %bitcast.63, f32[384]{0:T(512)S(1)} %get-tuple-element.22, bf16[16,768,128]{2,1,0:T(8,128)(2,1)} %get-tuple-element.11, ...), kind=kLoop, calls=%fused_computation.12 | loop fusion | flops 6291456 | bytes 6302724 | tf_op jit(solution)/shard_map/convert_element_type | solution.py:346
  88.6 1.9 %copy.26 = bf16[384,16,128]{0,2,1:T(8,128)(2,1)S(1)} copy(bf16[384,16,128]{2,0,1:T(8,128)(2,1)} %get-tuple-element.20) | data formatting | bytes 3145728 | tf_op jit(solution)/shard_map/convert_element_type | solution.py:346
  90.6 0.5 convolution_bitcast_fusion.1
  91.1 0.6 copy-done.10
  91.7 0.6 fusion.11.own_ref
  92.2 26.2 %hidden.1 = bf16[16,176,384]{2,1,0:T(8,128)(2,1)S(1)} custom-call(bf16[176,384]{1,0:T(8,128)(2,1)S(1)} %fusion.11.own_ref), custom_call_target="tpu_custom_call" | custom-call | tf_op jit(solution)/shard_map/hidden/pallas_call | solution.py:322
  118.5 1.0 fusion.9
  119.5 2.7 %copy.28 = bf16[384,16,128]{0,2,1:T(8,128)(2,1)} copy(bf16[384,16,128]{2,0,1:T(8,128)(2,1)} %get-tuple-element.19) | data formatting | bytes 3145728 | tf_op jit(solution)/shard_map/convert_element_type | solution.py:346
  122.3 2.5 %fusion.22 = f32[384,384]{0,1:T(8,128)S(1)} fusion(bf16[384,2048]{0,1:T(8,128)(2,1)} %bitcast.57, bf16[2048,384]{1,0:T(8,128)(2,1)S(1)} %bitcast.54), kind=kOutput, calls=%fused_computation.45 | convolution fusion | flops 603979776 | bytes 3735552 | tf_op jit(solution)/shard_map/dot_general | solution.py:430
  124.9 0.1 pad.12.clone
  125.0 0.7 fusion.8.part_ref
  125.7 18.4 %back.1 = bf16[384,128]{1,0:T(8,128)(2,1)S(1)} custom-call(s32[1,768]{1,0:T(1,128)S(1)} %bitcast.53, s32[1,1536]{1,0:T(1,128)S(1)} %reshape_reshape_squeeze.6.ids_ref, bf16[768,128]{1,0:T(8,128)(2,1)S(1)} %bitcast.51, bf16[16,384,128]{2,1,0:T(8,128)(2,1)S(1)} %fusion.8.part_ref), custom_call_target="tpu_custom_call" | custom-call | tf_op jit(solution)/shard_map/back/pallas_call | solution.py:322
  144.1 0.6 copy.39
  (38 shorter events, 0.3 us)
Async XLA Ops:
  0.0 118.4 %copy-start = (bf16[2,1408,128]{2,1,0:T(8,128)(2,1)S(1)}, bf16[2,1408,128]{2,1,0:T(8,128)(2,1)}, u32[]{:S(2)}) copy-start(bf16[2,1408,128]{2,1,0:T(8,128)(2,1)} %param.17) | copy-start | bytes 2162692
  15.2 0.9 copy-start.3
  16.1 32.4 %slice-start = ((bf16[64,176]{1,0:T(8,128)(2,1)}), bf16[64,128]{1,0:T(8,128)(2,1)S(1)}, s32[]{:S(2)}) async-start(bf16[64,176]{1,0:T(8,128)(2,1)} %param.12), calls=%async_computation | async-start | bytes 32768 | tf_op jit(solution)/shard_map/slice | solution.py:395
  16.1 32.4 %slice-start.1 = ((bf16[64,176]{1,0:T(8,128)(2,1)}), bf16[64,48]{1,0:T(8,128)(2,1)S(1)}, s32[]{:S(2)}) async-start(bf16[64,176]{1,0:T(8,128)(2,1)} %param.12), calls=%async_computation.1 | async-start | bytes 32768 | tf_op jit(solution)/shard_map/slice | solution.py:392
  16.1 32.5 %slice-start.2 = ((bf16[64,176]{1,0:T(8,128)(2,1)}), bf16[64,128]{1,0:T(8,128)(2,1)S(1)}, s32[]{:S(2)}) async-start(bf16[64,176]{1,0:T(8,128)(2,1)} %param.13), calls=%async_computation.2 | async-start | bytes 32768 | tf_op jit(solution)/shard_map/slice | solution.py:396
  16.2 32.5 %slice-start.3 = ((bf16[64,176]{1,0:T(8,128)(2,1)}), bf16[64,48]{1,0:T(8,128)(2,1)S(1)}, s32[]{:S(2)}) async-start(bf16[64,176]{1,0:T(8,128)(2,1)} %param.13), calls=%async_computation.3 | async-start | bytes 32768 | tf_op jit(solution)/shard_map/slice | solution.py:392
  48.0 0.8 copy-start.7
  48.4 36.0 %copy-start.8 = (f32[2048]{0:T(1024)S(1)}, f32[2048]{0:T(1024)}, u32[]{:S(2)}) copy-start(f32[2048]{0:T(1024)} %param.11) | copy-start | bytes 24580
  80.4 1.1 copy-start.1
  81.5 1.2 copy-start.4
  88.6 2.0 %copy-start.6 = (bf16[1,1,176,2048]{3,2,1,0:T(8,128)(2,1)S(1)}, bf16[1,1,176,2048]{3,2,1,0:T(8,128)(2,1)}, u32[]{:S(2)}) copy-start(bf16[1,1,176,2048]{3,2,1,0:T(8,128)(2,1)} %param.15) | copy-start | bytes 2162692
  90.5 1.1 copy-start.10
  92.2 26.2 %copy-start.9 = (f32[2,384]{1,0:T(2,128)S(1)}, f32[2,384]{1,0:T(2,128)}, u32[]{:S(2)}) copy-start(f32[2,384]{1,0:T(2,128)} %param.19) | copy-start | bytes 9220
  119.5 2.8 %copy-start.5 = (bf16[32,64,384]{2,1,0:T(8,128)(2,1)S(1)}, bf16[32,64,384]{2,1,0:T(8,128)(2,1)}, u32[]{:S(2)}) copy-start(bf16[32,64,384]{2,1,0:T(8,128)(2,1)} %copy-done.4) | copy-start | bytes 4718596
  122.2 2.7 %copy-start.2 = (bf16[32,64,256]{2,1,0:T(8,128)(2,1)S(1)}, bf16[32,64,256]{2,1,0:T(8,128)(2,1)}, u32[]{:S(2)}) copy-start(bf16[32,64,256]{2,1,0:T(8,128)(2,1)} %copy-done.1) | copy-start | bytes 3145732

commit v2 on v0

v2 whole, which is shorter than its diff:
```python
import jax
import jax.numpy as jnp
from jax import lax
from jax.experimental import pallas as pl
from jax.experimental.pallas import tpu as pltpu
from jax.sharding import PartitionSpec as P

MESH = pl.DeviceIdType.MESH
EXP_DEV = 2
TOK_DEV = 384
CAP = 384
NZ, NY, NX = 8, 8, 4
N_TP, N_EP = 16, 32
SLOT, ROOM = 24, 32
F_DEV, F = 176, 1408
D, W = 2048, 128
norm_eps = 1e-06
bf16, f32, i32 = jnp.bfloat16, jnp.float32, jnp.int32


class Link:
    def __init__(self, send_sems, recv_sems):
        self.send_sems, self.recv_sems = send_sems, recv_sems
        self.keys, self.sent = {}, []

    def _copy(self, src, dst, key, device):
        i = self.keys.setdefault(key, len(self.keys))
        return pltpu.make_async_remote_copy(
            src_ref=src,
            dst_ref=dst,
            send_sem=self.send_sems.at[i],
            recv_sem=self.recv_sems.at[i],
            device_id=device,
            device_id_type=MESH,
        )

    def send(self, src, dst, key, device):
        copy = self._copy(src, dst, key, device)
        copy.start()
        self.sent.append(copy)

    def arrive(self, dst, key, device):
        self._copy(dst, dst, key, device).wait_recv()

    def finish(self):
        for copy in self.sent:
            copy.wait_send()


def places():
    tp, ep = lax.axis_index("tp"), lax.axis_index("ep")
    return tp // 2, lax.rem(tp, 2), ep // NX, lax.rem(ep, NX)


def around(position, step, count):
    return lax.rem(position + step + count, count)


def z_device(z, core):
    return {"tp": z * 2 + core}


OFFSETS = sorted(
    [(a, b) for a in range(-3, 5) for b in range(-1, 3) if (a, b) != (0, 0)],
    key=lambda o: (o[1] % 4, o[0] % 8),
)


def greet():
    barrier = pltpu.get_barrier_semaphore()
    z, core, y, x = places()
    devices = [{"ep": around(y, a, NY) * NX + around(x, b, NX)} for a, b in OFFSETS]
    devices += [z_device(around(z, 1, NZ), core), z_device(around(z, -1, NZ), core)]
    devices += [z_device(z, 1 - core)]
    for device in devices:
        pl.semaphore_signal(barrier, inc=1, device_id=device, device_id_type=MESH)
    return len(devices)


class Exchange:
    def __init__(self, src, dst, src_all, dst_all, sems):
        self.src, self.dst, self.src_all, self.dst_all, self.sems = src, dst, src_all, dst_all, sems

    def start(self):
        _, _, y, x = places()
        own = y * NX + x
        for a, b in OFFSETS:
            peer = around(y, a, NY) * NX + around(x, b, NX)
            pltpu.make_async_remote_copy(
                src_ref=self.src(peer),
                dst_ref=self.dst(own),
                send_sem=self.sems.at[0],
                recv_sem=self.sems.at[1],
                device_id={"ep": peer},
                device_id_type=MESH,
            ).start()
        self.dst(own)[...] = self.src(own)[...]

    def arrive(self):
        part = self.dst_all
        pltpu.make_async_copy(part, part, self.sems.at[1]).wait()

    def finish(self):
        part = self.src_all
        pltpu.make_async_copy(part, part, self.sems.at[0]).wait()


def reach(direction, flipped):
    return 4 if (direction > 0) != bool(flipped) else 3


def ring_gather(pieces, link):
    z, core, _, _ = places()
    own = z * 2 + core
    other = z_device(z, 1 - core)
    beside = {d: z_device(around(z, d, NZ), core) for d in (1, -1)}
    for h, (flip, src, at) in enumerate(pieces):
        for d in (1, -1):
            link.send(src, at(own), (d, 1, h), beside[d])
    for h, (flip, src, at) in enumerate(pieces):
        link.send(src, at(own), ("core", 0, 0, h), other)
    for flip, src, at in pieces:
        at(own)[...] = src[...]
    yield
    for k in range(1, 5):
        for h, (flip, src, at) in enumerate(pieces):
            for d in (1, -1):
                most = reach(d, flip)
                if k > most:
                    continue
                block = at(around(z, -d * k, NZ) * 2 + core)
                link.arrive(block, (d, k, h), other)
                if k < most:
                    link.send(block, block, (d, k + 1, h), beside[d])
                link.send(block, block, ("core", d, k, h), other)
        yield
    for h, (flip, src, at) in enumerate(pieces):
        link.arrive(at(own + 1 - 2 * core), ("core", 0, 0, h), other)
        for k in range(1, 5):
            for d in (1, -1):
                if k <= reach(d, flip):
                    block = at(around(z, -d * k, NZ) * 2 + 1 - core)
                    link.arrive(block, ("core", d, k, h), other)
    yield


def plane_gather(src, dst, link, y_first):
    _, _, y, x = places()
    a, na, b, nb = (y, NY, x, NX) if y_first else (x, NX, y, NY)

    def index(p, q):
        return p * NX + q if y_first else q * NX + p

    own = index(a, b)
    here = {"ep": own}
    along = {d: {"ep": index(around(a, d, na), b)} for d in (1, -1)}
    across = {d: {"ep": index(a, around(b, d, nb))} for d in (1, -1)}
    for d in (1, -1):
        link.send(src, dst.at[own], ("a", d, 1), along[d])
    dst[own] = src[...]
    yield
    tags = [(0, 0)]
    for k in range(1, na // 2 + 1):
        for d in (1, -1):
            most = na // 2 if d > 0 else na // 2 - 1
            if k > most:
                continue
            tags.append((d, k))
            block = dst.at[index(around(a, -d * k, na), b)]
            link.arrive(block, ("a", d, k), here)
            if k < most:
                link.send(block, block, ("a", d, k + 1), along[d])
            yield
    for n, (d, k) in enumerate(tags):
        block = dst.at[index(around(a, -d * k, na), b)]
        for s in (1, -1):
            link.send(src if n == 0 else block, block, ("b", s, 1, n), across[s])
    yield
    for j in range(1, nb // 2 + 1):
        for n, (d, k) in enumerate(tags):
            for s in (1, -1):
                most = nb // 2 if (s > 0) == (n % 2 == 0) else nb // 2 - 1
                if j > most:
                    continue
                block = dst.at[index(around(a, -d * k, na), around(b, -s * j, nb))]
                link.arrive(block, ("b", s, j, n), here)
                if j < most:
                    link.send(block, block, ("b", s, j + 1, n), across[s])
                yield


def go(job, steps=1000):
    for _ in range(steps):
        if next(job, "end") == "end":
            return


def one_hot(condition):
    return jnp.where(condition, 1.0, 0.0).astype(bf16)


def silu(v):
    return v / (1.0 + jnp.exp(-v))


def dims(a, b):
    return (((a,), (b,)), ((), ()))


def normalise(blocks, gain_ref, out_ref):
    for r in range(0, TOK_DEV, W):
        rows = pl.ds(r, W)
        squares = jnp.zeros((W, W), f32)
        for t in range(N_TP):
            wide = blocks(t)[rows, :].astype(f32)
            squares = squares + wide * wide
        inv = lax.rsqrt(jnp.sum(squares, axis=1, keepdims=True) * (1.0 / D) + norm_eps)
        for t in range(N_TP):
            lanes = slice(t * W, (t + 1) * W)
            wide = blocks(t)[rows, :].astype(f32)
            out_ref[rows, lanes] = (wide * inv * gain_ref[:, lanes]).astype(bf16)


def layer_kernel(
    req_ref, col_ref, row_ref, tok_ref, gain_ref, gu_ref, dn_ref, gates_ref, eg_hbm, eu_hbm, ed_hbm,
    mixed_ref,
    asked, one_t, join, spread, out, came, tok_all, own, rows_all, wg, wd, hid, hid_all, back, returned,
    part, pair, got, made, eg, eu, ed, ed_t, normed, taken,
    load_sem, ask_sem, go_a, go_b, back_a, back_b,
    tok_s, tok_r, xa_s, xa_r, xb_s, xb_r, gu_s, gu_r, dn_s, dn_r, hid_s, hid_r, sum_s, sum_r,
):
    count = greet()
    z, core, _, _ = places()
    other = z_device(z, 1 - core)
    loads = [
        pltpu.make_async_copy(s, d, load_sem.at[i])
        for i, (s, d) in enumerate(((eg_hbm, eg), (eu_hbm, eu), (ed_hbm, ed)))
    ]
    for load in loads:
        load.start()
    came[...] = jnp.zeros_like(came)
    returned[...] = jnp.zeros_like(returned)
    for e in range(EXP_DEV):
        at = lax.broadcasted_iota(i32, (CAP, N_EP * ROOM), 1)
        join[e] = one_hot(at == col_ref[e])
    pl.semaphore_wait(pltpu.get_barrier_semaphore(), count)

    half = TOK_DEV // 2
    cuts = [pl.ds(0, half), pl.ds(half, half)]
    first = pl.ds(0, SLOT)
    some = pl.ds(0, N_EP - 1)

    ask = Exchange(
        lambda p: req_ref.at[p], lambda p: asked.at[p], req_ref.at[some], asked.at[some], ask_sem
    )
    ask.start()
    tok_link = Link(tok_s, tok_r)
    tok_ring = ring_gather(
        [(h, tok_ref.at[c], lambda t, c=c: tok_all.at[t, c]) for h, c in enumerate(cuts)], tok_link
    )
    go(tok_ring, 1)
    gu_link, dn_link = Link(gu_s, gu_r), Link(dn_s, dn_r)
    gu_job = plane_gather(gu_ref, wg, gu_link, True)
    dn_job = plane_gather(dn_ref, wd, dn_link, False)
    go(gu_job, 1)
    go(dn_job, 1)
    for e in range(EXP_DEV):
        at = lax.broadcasted_iota(i32, (N_EP * ROOM, CAP), 0)
        spread[e] = one_hot(at == row_ref[e])
    go(tok_ring, 1)
    go(gu_job, 2)
    go(dn_job, 2)

    ask.arrive()
    token = lax.broadcasted_iota(i32, (TOK_DEV, W), 0)
    for i in range(N_EP // 2):
        ids = jnp.maximum(asked[2 * i], asked[2 * i + 1])
        one_t[:, i * W : (i + 1) * W] = one_hot(token == ids)
    for i in range(4):
        lanes = slice(i * 512, (i + 1) * 512)
        picked = lax.dot_general(
            one_t[:, lanes], tok_ref[...], dims(0, 0), preferred_element_type=f32
        )
        out[i * 8 : (i + 1) * 8] = picked.astype(bf16).reshape(8, EXP_DEV, ROOM, W)
    dispatch = [
        Exchange(
            lambda p, e=e: out.at[p, e, first],
            lambda p, e=e: came.at[e, p, first],
            out.at[some, e, first],
            came.at[e, some, first],
            sem,
        )
        for e, sem in enumerate((go_a, go_b))
    ]
    for e in range(EXP_DEV):
        dispatch[e].start()
    go(tok_ring, 1)
    go(gu_job, 2)
    go(dn_job, 1)
    for load in loads:
        load.wait()
    for e in range(EXP_DEV):
        ed_t[e] = ed[e].T
    go(tok_ring, 1)
    go(gu_job, 2)

    x_links = [Link(xa_s, xa_r), Link(xb_s, xb_r)]
    x_rings = []
    for e in range(EXP_DEV):
        dispatch[e].arrive()
        own[e] = jnp.dot(
            join[e], came[e].reshape(N_EP * ROOM, W), preferred_element_type=f32
        ).astype(bf16)
        x_rings.append(
            ring_gather(
                [
                    (e + h, own.at[e, c], lambda t, c=c, e=e: rows_all.at[t, e, c])
                    for h, c in enumerate(cuts)
                ],
                x_links[e],
            )
        )
        go(x_rings[e], 1)
    go(tok_ring)
    go(gu_job, 2)
    go(dn_job, 1)
    for k in range(4):
        for e in range(EXP_DEV):
            go(x_rings[e], 1)
        if k > 0:
            go(gu_job, 6)
            go(dn_job, 6)
    for e in range(EXP_DEV):
        go(x_rings[e], 1)

    expert = z // (NZ // EXP_DEV)
    normalise(lambda t: rows_all.at[t, expert], gain_ref, taken)
    gate_values = lax.dot_general(eg[...], taken[...], dims(1, 1), preferred_element_type=f32)
    up_values = lax.dot_general(eu[...], taken[...], dims(1, 1), preferred_element_type=f32)
    hid[...] = (silu(gate_values) * up_values).astype(bf16)
    hid_link = Link(hid_s, hid_r)
    hid_ring = ring_gather(
        [
            (h, hid.at[c], lambda t, c=c: hid_all.at[t, c])
            for h, c in enumerate((pl.ds(0, 96), pl.ds(96, 80)))
        ],
        hid_link,
    )
    go(hid_ring, 1)

    normalise(lambda t: tok_all.at[t], gain_ref, normed)
    go(hid_ring, 1)
    go(gu_job)
    sums = jnp.dot(normed[...], wg[...].reshape(D, 384), preferred_element_type=f32)
    low = silu(sums[:, :W]) * sums[:, W : 2 * W]
    high = silu(sums[:, 256:304]) * sums[:, 304:352]
    shared = jnp.concatenate([low, high, jnp.zeros((TOK_DEV, 80), f32)], axis=1).astype(bf16)
    go(hid_ring, 1)
    go(dn_job)
    for t in range(N_TP):
        block = lax.dot_general(
            shared, wd[2 * t : 2 * t + 2].reshape(W, 256), dims(1, 1), preferred_element_type=f32
        )
        part[t] = block.astype(bf16)
    go(hid_ring, 1)

    link = Link(sum_s, sum_r)
    order = [4, -3, 3, -2, 2, -1, 1, 0]
    targets = {m % NZ: around(z, m, NZ) for m in order}
    for m in order:
        at = targets[m % NZ]
        link.send(part.at[at * 2 + 1 - core], pair.at[at], ("core", m % NZ), other)
    here = set()

    def term(m, rows):
        m = m % NZ
        at = targets[m]
        if m not in here:
            link.arrive(pair.at[at], ("core", m), other)
            here.add(m)
        return part[at * 2 + core, rows].astype(f32) + pair[at, rows].astype(f32)

    go(hid_ring)

    give = []
    for e in range(EXP_DEV):
        full = hid_all[e * 8 : (e + 1) * 8].reshape(F, CAP)
        outputs = jnp.dot(ed_t[e], full, preferred_element_type=f32)
        weighted = (outputs * gates_ref[e]).astype(bf16)
        slots = lax.dot_general(spread[e], weighted, dims(1, 1), preferred_element_type=f32)
        back[e] = slots.astype(bf16).reshape(N_EP, ROOM, W)
        give.append(
            Exchange(
                lambda p, e=e: back.at[e, p, first],
                lambda p, e=e: returned.at[p, e, first],
                back.at[e, some, first],
                returned.at[some, e, first],
                (back_a, back_b)[e],
            )
        )
        give[e].start()

    way = {1: 0, -1: 1}
    for k in range(1, 5):
        for h, rows in enumerate(cuts):
            for d in (1, -1):
                most = reach(d, h)
                if k > most:
                    continue
                total = term(d * (most + 1 - k), rows)
                if k > 1:
                    link.arrive(got.at[way[d], k - 1, rows], (d, k - 1, h), other)
                    total = total + got[way[d], k - 1, rows].astype(f32)
                made[way[d], k, rows] = total.astype(bf16)
                link.send(
                    made.at[way[d], k, rows],
                    got.at[way[d], k, rows],
                    (d, k, h),
                    z_device(around(z, d, NZ), core),
                )
    for e in range(EXP_DEV):
        give[e].arrive()
    routed = jnp.dot(one_t[...], returned[...].reshape(N_EP * 2 * ROOM, W), preferred_element_type=f32)
    for h, rows in enumerate(cuts):
        total = term(0, rows)
        for d in (1, -1):
            most = reach(d, h)
            link.arrive(got.at[way[d], most, rows], (d, most, h), other)
            total = total + got[way[d], most, rows].astype(f32)
        mixed_ref[rows, :] = (total + routed[h * half : (h + 1) * half]).astype(bf16)
    for one in (ask, *dispatch, *give):
        one.finish()
    for one in (tok_link, *x_links, gu_link, dn_link, hid_link, link):
        one.finish()


def requests_of(chosen):
    sources = chosen // TOK_DEV
    before = jnp.sum((sources[:, None, :] < sources[:, :, None]).astype(i32), axis=2)
    rank = jnp.arange(CAP, dtype=i32)[None, :] - before
    slots = sources * ROOM + rank
    local_ids = chosen - sources * TOK_DEV
    place = (
        jnp.arange(N_EP, dtype=i32)[:, None] * ROOM + jnp.arange(ROOM, dtype=i32)[None, :]
    )
    asked = jnp.max(
        jnp.where(place[None, :, :, None] == slots[:, None, None, :], local_ids[:, None, None, :], -1),
        axis=3,
    )
    asked = jnp.moveaxis(asked, 0, 1).reshape(N_EP, 1, EXP_DEV * ROOM)
    side = lax.rem(lax.axis_index("ep"), 2)
    lane = jnp.arange(W, dtype=i32)
    asked = jnp.where(lane // (W // 2) == side, jnp.concatenate([asked, asked], axis=2), -1)
    return slots, asked


def on_device(
    tokens,
    norm_gain,
    shared_gate,
    shared_up,
    shared_down,
    expert_gate,
    expert_up,
    expert_down,
    chosen,
    gates,
):
    slots, asked = requests_of(chosen)
    gu = jnp.concatenate(
        [shared_gate[:, :W], shared_up[:, :W], shared_gate[:, W:], shared_up[:, W:], jnp.zeros((64, 32), bf16)],
        axis=1,
    )
    dn = jnp.pad(shared_down.T, ((0, 0), (0, 80)))
    vmem = pl.BlockSpec(memory_space=pltpu.VMEM)
    hbm = pl.BlockSpec(memory_space=pl.ANY)
    pool = lambda *shape, dtype=bf16: pltpu.VMEM(shape, dtype)
    dma = lambda n: pltpu.SemaphoreType.DMA((n,))
    return pl.pallas_call(
        layer_kernel,
        name="layer",
        out_shape=jax.ShapeDtypeStruct((TOK_DEV, W), bf16),
        in_specs=[vmem] * 8 + [hbm] * 3,
        out_specs=vmem,
        scratch_shapes=[
            pool(N_EP, 1, W, dtype=i32),
            pool(TOK_DEV, N_EP * 2 * ROOM),
            pool(EXP_DEV, CAP, N_EP * ROOM),
            pool(EXP_DEV, N_EP * ROOM, CAP),
            pool(N_EP, EXP_DEV, ROOM, W),
            pool(EXP_DEV, N_EP, ROOM, W),
            pool(N_TP, TOK_DEV, W),
            pool(EXP_DEV, CAP, W),
            pool(N_TP, EXP_DEV, CAP, W),
            pool(N_EP, 64, 384),
            pool(N_EP, 64, 256),
            pool(F_DEV, CAP),
            pool(N_TP, F_DEV, CAP),
            pool(EXP_DEV, N_EP, ROOM, W),
            pool(N_EP, EXP_DEV, ROOM, W),
            pool(N_TP, TOK_DEV, W),
            pool(NZ, TOK_DEV, W),
            pool(2, 5, TOK_DEV, W),
            pool(2, 5, TOK_DEV, W),
            pool(F_DEV, D),
            pool(F_DEV, D),
            pool(EXP_DEV, F, W),
            pool(EXP_DEV, W, F),
            pool(TOK_DEV, D),
            pool(CAP, D),
            dma(3),
            *[dma(2)] * 5,
            *[dma(32)] * 14,
        ],
        compiler_params=pltpu.CompilerParams(
            collective_id=0, has_side_effects=True, vmem_limit_bytes=56 * 1024 * 1024
        ),
    )(
        asked,
        slots.reshape(EXP_DEV, CAP, 1),
        slots.reshape(EXP_DEV, 1, CAP),
        tokens,
        norm_gain.reshape(1, D),
        gu,
        dn,
        gates.reshape(EXP_DEV, 1, CAP),
        expert_gate.reshape(F_DEV, D),
        expert_up.reshape(F_DEV, D),
        expert_down,
    )


def solution(mesh):
    return jax.shard_map(
        on_device,
        mesh=mesh,
        in_specs=(
            P("ep", "tp"),
            P(),
            P("ep", "tp"),
            P("ep", "tp"),
            P("tp", "ep"),
            P("tp", "ep", None, None),
            P("tp", "ep", None, None),
            P("ep", None, "tp"),
            P("ep", None),
            P("ep", None),
        ),
        out_specs=P("ep", "tp"),
        check_vma=False,
    )
```

time: 286 us -> 109 us (0.38)
  waiting for transfers between devices: 149 us -> 0 us
  Pallas kernels: 0 us -> 96.1 us
  local copies, waits for them, and re-layouts: 60.1 us -> 9.43 us
  starting transfers between devices: 31.4 us -> 0 us
  matrix products: 18.4 us -> 0 us
  between operations: 15.2 us -> 0.04 us
  other arithmetic: 9.57 us -> 3.11 us
    all_to_all x4 -> x0, waiting for transfers between devices: 96.3 us -> none  [the longest x1 71.4 us: on_device(): lax.all_to_all(outgoing, 'ep', split_axis=0, concat_axis=0, tiled=True)]
    pallas_call x0 -> x1, Pallas kernels: none -> 96.1 us  [on_device(): pl.pallas_call(layer_kernel, name='layer', out_shape=jax.ShapeDtypeStruct...]
    scatter x3 -> x0, local copies, waits for them, and re-layouts: 42.5 us -> none  [the longest x1 36.5 us: on_device(): requests = jnp.full((EXP_DEV, slot_count), TOK_DEV, jnp.int32).at[expert_...]
    all_to_all x4 -> x0, starting transfers between devices: 31.2 us -> none  [the longest x1 10.5 us: on_device(): lax.all_to_all(requests, 'ep', split_axis=1, concat_axis=1, tiled=True)]
    all_gather x3 -> x0, waiting for transfers between devices: 26.9 us -> none  [the longest x1 20.1 us: on_device(): all_hidden = lax.all_gather(part_hidden, 'tp', axis=0, tiled=True)]
    unnamed x5 -> x0, waiting for transfers between devices: 25.4 us -> none
    dot_general x7 -> x0, matrix products: 18.4 us -> none  [the longest x1 4.28 us: on_device(): jnp.dot(shared_hidden, gathered_copies(shared_down, 'ep', 1), preferred_e...]
    gather x4 -> x0, local copies, waits for them, and re-layouts: 10.9 us -> none  [the longest x3 6.63 us: on_device(): run_start = jnp.take_along_axis(starts, sources, axis=1)]
  transfers between devices with their start and end apart: 8 -> 0, of which waited for: 6 -> 0; matrix products, arithmetic and copies ran while one was open for 27% -> 0% of each run, Pallas kernels for 0% -> 0%
where the time goes in v2:
time: 109 us
  Pallas kernels  96.1 us (88%)
  local copies, waits for them, and re-layouts  9.43 us (9%)
  other arithmetic  3.11 us (3%)
    pallas_call x1, Pallas kernels, on_device(): pl.pallas_call(layer_kernel, name='layer', out_shape=jax.ShapeDtypeStruct...  96.1 us

profile of v2, /device:TPU:1, one launch (start us, length us, event | category | flops | bytes accessed | tf_op | source)
XLA Modules:
  0.0 108.7 jit_solution(17004120297949490955)
XLA Ops:
  0.0 1.3 %reshape.105.gates_ref = f32[2,1,384]{2,1,0:T(1,128)} reshape(f32[2,384]{1,0:T(2,128)} %param.19) | data formatting | bytes 6144 | tf_op jit(solution)/shard_map/reshape | solution.py:526
  1.3 0.7 multiply_subtract_fusion
  2.0 0.3 convert_reduce_fusion
  2.3 0.6 reshape.103.row_ref
  2.9 0.1 iota_add_fusion
  3.0 1.3 %select_reduce_fusion = s32[2,32,32]{2,1,0:T(8,128)S(1)} fusion(s32[2,384]{1,0:T(2,128)S(1)} %get-tuple-element.5, s32[2,384]{1,0:T(2,128)S(1)} %subtract_add_fusion, s32[32,32]{1,0:T(8,128)S(1)} %iota_add_fusion), kind=kLoop, calls=%fused_computation | loop fusion | flops 2357248 | bytes 18432 | tf_op jit(solution)/shard_map/reduce_max | solution.py:446
  4.3 0.1 concatenate.16
  4.4 0.7 broadcast_select_fusion.req_ref
  5.1 0.7 slice.14
  5.9 0.7 slice.12
  6.6 0.7 slice.15
  7.3 0.7 slice.13
  8.0 0.7 concatenate.18.gu_ref
  8.7 1.4 %pad.4.dn_ref = bf16[64,256]{1,0:T(8,128)(2,1)} pad(bf16[64,176]{1,0:T(8,128)(2,1)} %bitcast.10, bf16[]{:T(256)} %constant.43.clone.1), padding=0_0x0_80 | pad | bytes 55298 | tf_op jit(solution)/shard_map/jit(_pad)/pad | solution.py:474
  10.1 0.9 copy.13.col_ref
  11.0 96.1 %layer.1 = bf16[384,128]{1,0:T(8,128)(2,1)} custom-call(s32[32,1,128]{2,1,0:T(1,128)} %broadcast_select_fusion.req_ref, s32[2,384,1]{2,1,0:T(8,128)} %copy.13.col_ref, s32[2,1,384]{2,1,0:T(1,128)} %reshape.103.row_ref, bf16[384,128]{1,0:T(8,128)(2,1)} %tok_ref.1, f32[1,2048]{1,0:T(1,128)} %bitcast.11, bf16[64,384]{1,0:T(8,128)(2,1)} %concatenate.18.gu_ref, ...), custom_call_target="tpu_custom_call" | custom-call | tf_op jit(solution)/shard_map/layer/pallas_call | solution.py:479
  107.1 1.5 %copy.15 = bf16[384,128]{1,0:T(8,128)(2,1)} copy(bf16[384,128]{1,0:T(8,128)(2,1)} %layer.1) | data formatting | bytes 196608
  (5 shorter events, 0.1 us)

commit v3 on v2

--- a/solution.py
+++ b/solution.py
@@ -222,9 +222,9 @@
 
 
 def layer_kernel(
-    req_ref, col_ref, row_ref, tok_ref, gain_ref, gu_ref, dn_ref, gates_ref, eg_hbm, eu_hbm, ed_hbm,
+    chosen_ref, tok_ref, gain_ref, sg_ref, su_ref, sd_ref, gates_ref, eg_hbm, eu_hbm, ed_hbm,
     mixed_ref,
-    asked, one_t, join, spread, out, came, tok_all, own, rows_all, wg, wd, hid, hid_all, back, returned,
+    req_ref, gu_ref, dn_ref, wanted, asked, one_t, join, spread, out, came, tok_all, own, rows_all, wg, wd, hid, hid_all, back, returned,
     part, pair, got, made, eg, eu, ed, ed_t, normed, taken,
     load_sem, ask_sem, go_a, go_b, back_a, back_b,
     tok_s, tok_r, xa_s, xa_r, xb_s, xb_r, gu_s, gu_r, dn_s, dn_r, hid_s, hid_r, sum_s, sum_r,
@@ -238,11 +238,40 @@
     ]
     for load in loads:
         load.start()
+    gu_ref[:, :W] = sg_ref[:, :W]
+    gu_ref[:, W : 2 * W] = su_ref[:, :W]
+    gu_ref[:, 2 * W :] = jnp.concatenate(
+        [sg_ref[:, W:], su_ref[:, W:], jnp.zeros((64, 32), bf16)], axis=1
+    )
+    dn_ref[...] = jnp.concatenate([sd_ref[...], jnp.zeros((64, 80), bf16)], axis=1)
     came[...] = jnp.zeros_like(came)
     returned[...] = jnp.zeros_like(returned)
-    for e in range(EXP_DEV):
-        at = lax.broadcasted_iota(i32, (CAP, N_EP * ROOM), 1)
-        join[e] = one_hot(at == col_ref[e])
+    slot_rows = []
+    lane = lax.broadcasted_iota(i32, (CAP, W), 1)
+    for e in range(EXP_DEV):
+        ids = chosen_ref[e : e + 1, :]
+        sources = owner_of(ids)
+        ids_down = jnp.broadcast_to(ids, (W, CAP)).T
+        sources_down = owner_of(ids_down)
+        before = jnp.sum(
+            jnp.where(jnp.concatenate([sources_down] * 3, axis=1) < sources, 1, 0), axis=0, keepdims=True
+        )
+        slots = sources * ROOM + lax.broadcasted_iota(i32, (1, CAP), 1) - before
+        slot_rows.append(slots)
+        slots_down = jnp.broadcast_to(slots, (W, CAP)).T
+        local = ids_down - sources_down * TOK_DEV
+        for b in range(N_EP * ROOM // W):
+            match = slots_down == lane + b * W
+            join[e, :, b * W : (b + 1) * W] = one_hot(match)
+            wanted[e, b : b + 1] = jnp.max(jnp.where(match, local, -1), axis=0, keepdims=True)
+    side = lax.rem(lax.axis_index("ep"), 2)
+    lane = lax.broadcasted_iota(i32, (NY, W), 1)
+    for i in range(NX):
+        a, b = (pltpu.roll(wanted[e], (e - i) % NX * ROOM, 1) for e in range(EXP_DEV))
+        both = jnp.where(lane < ROOM, a, jnp.where(lane < 2 * ROOM, b, -1))
+        both = jnp.where(side == 0, both, pltpu.roll(both, W // 2, 1))
+        for j in range(NY):
+            req_ref[j * NX + i] = both[j : j + 1]
     pl.semaphore_wait(pltpu.get_barrier_semaphore(), count)
 
     half = TOK_DEV // 2
@@ -266,7 +295,7 @@
     go(dn_job, 1)
     for e in range(EXP_DEV):
         at = lax.broadcasted_iota(i32, (N_EP * ROOM, CAP), 0)
-        spread[e] = one_hot(at == row_ref[e])
+        spread[e] = one_hot(at == slot_rows[e])
     go(tok_ring, 1)
     go(gu_job, 2)
     go(dn_job, 2)
@@ -386,7 +415,7 @@
     for e in range(EXP_DEV):
         full = hid_all[e * 8 : (e + 1) * 8].reshape(F, CAP)
         outputs = jnp.dot(ed_t[e], full, preferred_element_type=f32)
-        weighted = (outputs * gates_ref[e]).astype(bf16)
+        weighted = (outputs * gates_ref[e : e + 1, :]).astype(bf16)
         slots = lax.dot_general(spread[e], weighted, dims(1, 1), preferred_element_type=f32)
         back[e] = slots.astype(bf16).reshape(N_EP, ROOM, W)
         give.append(
@@ -427,31 +456,15 @@
             most = reach(d, h)
             link.arrive(got.at[way[d], most, rows], (d, most, h), other)
             total = total + got[way[d], most, rows].astype(f32)
-        mixed_ref[rows, :] = (total + routed[h * half : (h + 1) * half]).astype(bf16)
+        mixed_ref[rows, :] = total + routed[h * half : (h + 1) * half]
     for one in (ask, *dispatch, *give):
         one.finish()
     for one in (tok_link, *x_links, gu_link, dn_link, hid_link, link):
         one.finish()
 
 
-def requests_of(chosen):
-    sources = chosen // TOK_DEV
-    before = jnp.sum((sources[:, None, :] < sources[:, :, None]).astype(i32), axis=2)
-    rank = jnp.arange(CAP, dtype=i32)[None, :] - before
-    slots = sources * ROOM + rank
-    local_ids = chosen - sources * TOK_DEV
-    place = (
-        jnp.arange(N_EP, dtype=i32)[:, None] * ROOM + jnp.arange(ROOM, dtype=i32)[None, :]
-    )
-    asked = jnp.max(
-        jnp.where(place[None, :, :, None] == slots[:, None, None, :], local_ids[:, None, None, :], -1),
-        axis=3,
-    )
-    asked = jnp.moveaxis(asked, 0, 1).reshape(N_EP, 1, EXP_DEV * ROOM)
-    side = lax.rem(lax.axis_index("ep"), 2)
-    lane = jnp.arange(W, dtype=i32)
-    asked = jnp.where(lane // (W // 2) == side, jnp.concatenate([asked, asked], axis=2), -1)
-    return slots, asked
+def owner_of(ids):
+    return ((ids >> 7) * 171) >> 9
 
 
 def on_device(
@@ -466,12 +479,6 @@
     chosen,
     gates,
 ):
-    slots, asked = requests_of(chosen)
-    gu = jnp.concatenate(
-        [shared_gate[:, :W], shared_up[:, :W], shared_gate[:, W:], shared_up[:, W:], jnp.zeros((64, 32), bf16)],
-        axis=1,
-    )
-    dn = jnp.pad(shared_down.T, ((0, 0), (0, 80)))
     vmem = pl.BlockSpec(memory_space=pltpu.VMEM)
     hbm = pl.BlockSpec(memory_space=pl.ANY)
     pool = lambda *shape, dtype=bf16: pltpu.VMEM(shape, dtype)
@@ -479,10 +486,14 @@
     return pl.pallas_call(
         layer_kernel,
         name="layer",
-        out_shape=jax.ShapeDtypeStruct((TOK_DEV, W), bf16),
-        in_specs=[vmem] * 8 + [hbm] * 3,
+        out_shape=jax.ShapeDtypeStruct((TOK_DEV, W), f32),
+        in_specs=[vmem] * 7 + [hbm] * 3,
         out_specs=vmem,
         scratch_shapes=[
+            pool(N_EP, 1, W, dtype=i32),
+            pool(64, 384),
+            pool(64, 256),
+            pool(EXP_DEV, NY, W, dtype=i32),
             pool(N_EP, 1, W, dtype=i32),
             pool(TOK_DEV, N_EP * 2 * ROOM),
             pool(EXP_DEV, CAP, N_EP * ROOM),
@@ -516,18 +527,17 @@
             collective_id=0, has_side_effects=True, vmem_limit_bytes=56 * 1024 * 1024
         ),
     )(
-        asked,
-        slots.reshape(EXP_DEV, CAP, 1),
-        slots.reshape(EXP_DEV, 1, CAP),
+        chosen,
         tokens,
         norm_gain.reshape(1, D),
-        gu,
-        dn,
-        gates.reshape(EXP_DEV, 1, CAP),
+        shared_gate,
+        shared_up,
+        shared_down.T,
+        gates,
         expert_gate.reshape(F_DEV, D),
         expert_up.reshape(F_DEV, D),
         expert_down,
-    )
+    ).astype(bf16)
 
 
 def solution(mesh):

time: 109 us -> 97.8 us (0.90)
  local copies, waits for them, and re-layouts: 9.43 us -> 0 us
  other arithmetic: 3.11 us -> 1.58 us
    slice x4 -> x0, local copies, waits for them, and re-layouts: 2.87 us -> none  [the longest x1 0.72 us: on_device(): shared_gate[:, W:]]
    reshape x3 -> x0, local copies, waits for them, and re-layouts: 2.8 us -> none  [the longest x1 1.28 us: on_device(): gates.reshape(EXP_DEV, 1, CAP)]
    convert_element_type x0 -> x1, other arithmetic: none -> 1.58 us  [on_device(): return pl.pallas_call(layer_kernel, name='layer', out_shape=jax.ShapeDtyp...]
    unnamed x1 -> x0, local copies, waits for them, and re-layouts: 1.54 us -> none
    pad x1 -> x0, local copies, waits for them, and re-layouts: 1.36 us -> none  [on_device(): dn = jnp.pad(shared_down.T, ((0, 0), (0, 80)))]
    reduce_max x1 -> x0, other arithmetic: 1.32 us -> none  [requests_of(): jnp.max(jnp.where(place[None, :, :, None] == slots[:, None, None, :], loc...]
where the time goes in v3:
time: 97.8 us; the launch traced here: 97.7 us
  Pallas kernels  96.1 us (98%)
  other arithmetic  1.58 us (2%)
    pallas_call x1, Pallas kernels, on_device(): pl.pallas_call(layer_kernel, name='layer', out_shape=jax.ShapeDtypeStruct...  96.1 us

profile of v3, /device:TPU:1, one launch (start us, length us, event | category | flops | bytes accessed | tf_op | source)
XLA Modules:
  0.0 97.7 jit_solution(6914384201976028055)
XLA Ops:
  0.0 96.1 %layer.1 = f32[384,128]{1,0:T(8,128)} custom-call(s32[2,384]{1,0:T(2,128)} %chosen_ref.1, bf16[384,128]{1,0:T(8,128)(2,1)} %tok_ref.1, f32[1,2048]{1,0:T(1,128)} %bitcast.7, bf16[64,176]{1,0:T(8,128)(2,1)} %sg_ref.1, bf16[64,176]{1,0:T(8,128)(2,1)} %su_ref.1, bf16[64,176]{1,0:T(8,128)(2,1)} %bitcast.6, f32[2,384]{1,0:T(2,128)} %gates_ref.1, ...), custom_call_target="tpu_custom_call" | custom-call | tf_op jit(solution)/shard_map/layer/pallas_call | solution.py:486
  96.1 1.6 %convert_element_type.3 = bf16[384,128]{1,0:T(8,128)(2,1)} convert(f32[384,128]{1,0:T(8,128)} %layer.1) | non-fusion elementwise | flops 49152 | bytes 294912 | tf_op jit(solution)/shard_map/convert_element_type | solution.py:540

commit v4 on v3

--- a/solution.py
+++ b/solution.py
@@ -21,7 +21,7 @@
 class Link:
     def __init__(self, send_sems, recv_sems):
         self.send_sems, self.recv_sems = send_sems, recv_sems
-        self.keys, self.sent = {}, []
+        self.keys, self.sent = {}, {None: [], 0: [], 1: []}
 
     def _copy(self, src, dst, key, device):
         i = self.keys.setdefault(key, len(self.keys))
@@ -34,17 +34,26 @@
             device_id_type=MESH,
         )
 
-    def send(self, src, dst, key, device):
-        copy = self._copy(src, dst, key, device)
-        copy.start()
-        self.sent.append(copy)
+    def send(self, copy, core=None):
+        self._copy(*copy()).start()
+        self.sent[core].append(copy)
 
     def arrive(self, dst, key, device):
         self._copy(dst, dst, key, device).wait_recv()
 
     def finish(self):
-        for copy in self.sent:
-            copy.wait_send()
+        for copy in self.sent[None]:
+            self._copy(*copy()).wait_send()
+        for core in (0, 1):
+
+            @on_core(core)
+            def _(core=core):
+                for copy in self.sent[core]:
+                    self._copy(*copy()).wait_send()
+
+
+def on_core(core):
+    return pl.when(lax.rem(lax.axis_index("tp"), 2) == core)
 
 
 def places():
@@ -110,83 +119,152 @@
 
 
 def ring_gather(pieces, link):
-    z, core, _, _ = places()
-    own = z * 2 + core
-    other = z_device(z, 1 - core)
-    beside = {d: z_device(around(z, d, NZ), core) for d in (1, -1)}
-    for h, (flip, src, at) in enumerate(pieces):
-        for d in (1, -1):
-            link.send(src, at(own), (d, 1, h), beside[d])
-    for h, (flip, src, at) in enumerate(pieces):
-        link.send(src, at(own), ("core", 0, 0, h), other)
+    def place():
+        return lax.axis_index("tp") // 2
+
+    def beside(d):
+        return z_device(around(place(), d, NZ), 1)
+
+    def mate(core):
+        return z_device(place(), core)
+
+    numbered = list(enumerate(pieces))
+    order = [(c, h, (flip + c) % 2, at) for c in (1, 0) for h, (flip, src, at) in numbered]
+
+    @on_core(1)
+    def _():
+        for h, (flip, src, at) in numbered:
+            for d in (1, -1):
+                link.send(lambda h=h, src=src, at=at, d=d: (src, at(place() * 2 + 1), (d, 1, h, 1), beside(d)), 1)
+        for h, (flip, src, at) in numbered:
+            link.send(lambda h=h, src=src, at=at: (src, at(place() * 2 + 1), ("core", 0, 0, h, 1), mate(0)), 1)
+
+    @on_core(0)
+    def _():
+        for h, (flip, src, at) in numbered:
+            link.send(lambda h=h, src=src, at=at: (src, at(place() * 2), ("core", 0, 0, h, 0), mate(1)), 0)
+
     for flip, src, at in pieces:
-        at(own)[...] = src[...]
+        at(lax.axis_index("tp"))[...] = src[...]
+
+    @on_core(1)
+    def _():
+        for h, (flip, src, at) in numbered:
+            block = lambda at=at: at(place() * 2)
+            link.arrive(block(), ("core", 0, 0, h, 0), mate(0))
+            for d in (1, -1):
+                link.send(lambda h=h, b=block, d=d: (b(), b(), (d, 1, h, 0), beside(d)), 1)
+
     yield
     for k in range(1, 5):
-        for h, (flip, src, at) in enumerate(pieces):
-            for d in (1, -1):
-                most = reach(d, flip)
-                if k > most:
-                    continue
-                block = at(around(z, -d * k, NZ) * 2 + core)
-                link.arrive(block, (d, k, h), other)
-                if k < most:
-                    link.send(block, block, (d, k + 1, h), beside[d])
-                link.send(block, block, ("core", d, k, h), other)
+
+        @on_core(1)
+        def _(k=k):
+            for c, h, flip, at in order:
+                for d in (1, -1):
+                    most = reach(d, flip)
+                    if k > most:
+                        continue
+                    block = lambda at=at, d=d, c=c: at(around(place(), -d * k, NZ) * 2 + c)
+                    link.arrive(block(), (d, k, h, c), mate(0))
+                    if k < most:
+                        link.send(lambda b=block, d=d, h=h, c=c: (b(), b(), (d, k + 1, h, c), beside(d)), 1)
+                    link.send(lambda b=block, d=d, h=h, c=c: (b(), b(), ("core", d, k, h, c), mate(0)), 1)
+
         yield
-    for h, (flip, src, at) in enumerate(pieces):
-        link.arrive(at(own + 1 - 2 * core), ("core", 0, 0, h), other)
+
+    @on_core(0)
+    def _():
+        for h, (flip, src, at) in numbered:
+            link.arrive(at(place() * 2 + 1), ("core", 0, 0, h, 1), mate(1))
         for k in range(1, 5):
-            for d in (1, -1):
-                if k <= reach(d, flip):
-                    block = at(around(z, -d * k, NZ) * 2 + 1 - core)
-                    link.arrive(block, ("core", d, k, h), other)
+            for c, h, flip, at in order:
+                for d in (1, -1):
+                    if k <= reach(d, flip):
+                        link.arrive(at(around(place(), -d * k, NZ) * 2 + c), ("core", d, k, h, c), mate(1))
+
     yield
 
 
 def plane_gather(src, dst, link, y_first):
-    _, _, y, x = places()
-    a, na, b, nb = (y, NY, x, NX) if y_first else (x, NX, y, NY)
-
-    def index(p, q):
-        return p * NX + q if y_first else q * NX + p
-
-    own = index(a, b)
-    here = {"ep": own}
-    along = {d: {"ep": index(around(a, d, na), b)} for d in (1, -1)}
-    across = {d: {"ep": index(a, around(b, d, nb))} for d in (1, -1)}
-    for d in (1, -1):
-        link.send(src, dst.at[own], ("a", d, 1), along[d])
-    dst[own] = src[...]
+    na, nb = (NY, NX) if y_first else (NX, NY)
+
+    def at(da=0, db=0):
+        _, _, y, x = places()
+        if y_first:
+            return around(y, da, NY) * NX + around(x, db, NX)
+        return around(y, db, NY) * NX + around(x, da, NX)
+
+    def mate(core):
+        return z_device(places()[0], core)
+
+    def send(key, da, db, block):
+        link.send(lambda: (block(), block(), key, {"ep": at(da, db)}), 0)
+
+    @on_core(1)
+    def _():
+        link.send(lambda: (src, dst.at[at(), 1], ("in",), mate(0)), 1)
+
+    dst[at(), lax.rem(lax.axis_index("tp"), 2)] = src[...]
+    yield
+
+    @on_core(0)
+    def _():
+        link.arrive(dst.at[at(), 1], ("in",), mate(1))
+        for d in (1, -1):
+            send(("a", d, 1), d, 0, lambda: dst.at[at()])
+        for s in (1, -1):
+            send(("b", s, 1, 0), 0, s, lambda: dst.at[at()])
+
     yield
     tags = [(0, 0)]
+    to_one = []
+
+    def share(block, key):
+        to_one.append((block, key))
+        link.send(lambda: (block().at[1], block().at[1], key, mate(1)), 0)
+
     for k in range(1, na // 2 + 1):
         for d in (1, -1):
             most = na // 2 if d > 0 else na // 2 - 1
             if k > most:
                 continue
+            block = lambda d=d, k=k: dst.at[at(-d * k, 0)]
+
+            @on_core(0)
+            def _(d=d, k=k, block=block):
+                link.arrive(block(), ("a", d, k), {"ep": at()})
+                if k < most:
+                    send(("a", d, k + 1), d, 0, block)
+                for s in (1, -1):
+                    send(("b", s, 1, len(tags)), 0, s, block)
+                share(block, ("one", len(to_one)))
+
             tags.append((d, k))
-            block = dst.at[index(around(a, -d * k, na), b)]
-            link.arrive(block, ("a", d, k), here)
-            if k < most:
-                link.send(block, block, ("a", d, k + 1), along[d])
             yield
-    for n, (d, k) in enumerate(tags):
-        block = dst.at[index(around(a, -d * k, na), b)]
-        for s in (1, -1):
-            link.send(src if n == 0 else block, block, ("b", s, 1, n), across[s])
-    yield
     for j in range(1, nb // 2 + 1):
         for n, (d, k) in enumerate(tags):
             for s in (1, -1):
                 most = nb // 2 if (s > 0) == (n % 2 == 0) else nb // 2 - 1
                 if j > most:
                     continue
-                block = dst.at[index(around(a, -d * k, na), around(b, -s * j, nb))]
-                link.arrive(block, ("b", s, j, n), here)
-                if j < most:
-                    link.send(block, block, ("b", s, j + 1, n), across[s])
+                block = lambda d=d, k=k, s=s, j=j: dst.at[at(-d * k, -s * j)]
+
+                @on_core(0)
+                def _(s=s, j=j, n=n, block=block):
+                    link.arrive(block(), ("b", s, j, n), {"ep": at()})
+                    if j < most:
+                        send(("b", s, j + 1, n), 0, s, block)
+                    share(block, ("one", len(to_one)))
+
                 yield
+
+    @on_core(1)
+    def _():
+        for block, key in to_one:
+            link.arrive(block().at[1], key, mate(0))
+
+    yield
 
 
 def go(job, steps=1000):
@@ -222,8 +300,9 @@
 
 
 def layer_kernel(
-    chosen_ref, tok_ref, gain_ref, sg_ref, su_ref, sd_ref, gates_ref, eg_hbm, eu_hbm, ed_hbm,
+    chosen_hbm, sg_hbm, su_hbm, sd_hbm, tok_hbm, gain_hbm, gates_hbm, eg_hbm, eu_hbm, ed_hbm,
     mixed_ref,
+    chosen_ref, sg_ref, su_ref, sd_ref, tok_ref, gain_ref, gates_ref,
     req_ref, gu_ref, dn_ref, wanted, asked, one_t, join, spread, out, came, tok_all, own, rows_all, wg, wd, hid, hid_all, back, returned,
     part, pair, got, made, eg, eu, ed, ed_t, normed, taken,
     load_sem, ask_sem, go_a, go_b, back_a, back_b,
@@ -234,10 +313,25 @@
     other = z_device(z, 1 - core)
     loads = [
         pltpu.make_async_copy(s, d, load_sem.at[i])
-        for i, (s, d) in enumerate(((eg_hbm, eg), (eu_hbm, eu), (ed_hbm, ed)))
+        for i, (s, d) in enumerate(
+            (
+                (chosen_hbm, chosen_ref),
+                (sg_hbm, sg_ref),
+                (su_hbm, su_ref),
+                (sd_hbm, sd_ref),
+                (tok_hbm, tok_ref),
+                (gain_hbm, gain_ref),
+                (gates_hbm, gates_ref),
+                (eg_hbm, eg),
+                (eu_hbm, eu),
+                (ed_hbm, ed),
+            )
+        )
     ]
     for load in loads:
         load.start()
+    for load in loads[:4]:
+        load.wait()
     gu_ref[:, :W] = sg_ref[:, :W]
     gu_ref[:, W : 2 * W] = su_ref[:, :W]
     gu_ref[:, 2 * W :] = jnp.concatenate(
@@ -272,6 +366,7 @@
         both = jnp.where(side == 0, both, pltpu.roll(both, W // 2, 1))
         for j in range(NY):
             req_ref[j * NX + i] = both[j : j + 1]
+    loads[4].wait()
     pl.semaphore_wait(pltpu.get_barrier_semaphore(), count)
 
     half = TOK_DEV // 2
@@ -279,6 +374,10 @@
     first = pl.ds(0, SLOT)
     some = pl.ds(0, N_EP - 1)
 
+    half = TOK_DEV // 2
+    cuts = [pl.ds(0, half), pl.ds(half, half)]
+    first = pl.ds(0, SLOT)
+    some = pl.ds(0, N_EP - 1)
     ask = Exchange(
         lambda p: req_ref.at[p], lambda p: asked.at[p], req_ref.at[some], asked.at[some], ask_sem
     )
@@ -297,8 +396,6 @@
         at = lax.broadcasted_iota(i32, (N_EP * ROOM, CAP), 0)
         spread[e] = one_hot(at == slot_rows[e])
     go(tok_ring, 1)
-    go(gu_job, 2)
-    go(dn_job, 2)
 
     ask.arrive()
     token = lax.broadcasted_iota(i32, (TOK_DEV, W), 0)
@@ -323,15 +420,12 @@
     ]
     for e in range(EXP_DEV):
         dispatch[e].start()
-    go(tok_ring, 1)
-    go(gu_job, 2)
-    go(dn_job, 1)
-    for load in loads:
+    for load in loads[5:]:
         load.wait()
     for e in range(EXP_DEV):
         ed_t[e] = ed[e].T
     go(tok_ring, 1)
-    go(gu_job, 2)
+    go(tok_ring, 1)
 
     x_links = [Link(xa_s, xa_r), Link(xb_s, xb_r)]
     x_rings = []
@@ -350,15 +444,14 @@
             )
         )
         go(x_rings[e], 1)
-    go(tok_ring)
-    go(gu_job, 2)
-    go(dn_job, 1)
+        if e == 0:
+            go(tok_ring, 1)
+    for k in range(13):
+        go(gu_job, 1)
+        go(dn_job, 1)
     for k in range(4):
         for e in range(EXP_DEV):
             go(x_rings[e], 1)
-        if k > 0:
-            go(gu_job, 6)
-            go(dn_job, 6)
     for e in range(EXP_DEV):
         go(x_rings[e], 1)
 
@@ -377,38 +470,56 @@
     )
     go(hid_ring, 1)
 
+    for k in range(18):
+        go(gu_job, 1)
+        go(dn_job, 1)
+    go(tok_ring)
     normalise(lambda t: tok_all.at[t], gain_ref, normed)
     go(hid_ring, 1)
+    go(hid_ring, 1)
     go(gu_job)
-    sums = jnp.dot(normed[...], wg[...].reshape(D, 384), preferred_element_type=f32)
+    mine = pl.ds(core, 1)
+    weights = wg[:, mine].reshape(D, 384)
+    sums = jnp.dot(normed[...], weights, preferred_element_type=f32)
     low = silu(sums[:, :W]) * sums[:, W : 2 * W]
     high = silu(sums[:, 256:304]) * sums[:, 304:352]
     shared = jnp.concatenate([low, high, jnp.zeros((TOK_DEV, 80), f32)], axis=1).astype(bf16)
     go(hid_ring, 1)
     go(dn_job)
+    link = Link(sum_s, sum_r)
     for t in range(N_TP):
-        block = lax.dot_general(
-            shared, wd[2 * t : 2 * t + 2].reshape(W, 256), dims(1, 1), preferred_element_type=f32
-        )
+        weights = wd[2 * t : 2 * t + 2, mine].reshape(W, 256)
+        block = lax.dot_general(shared, weights, dims(1, 1), preferred_element_type=f32)
         part[t] = block.astype(bf16)
+        if t % 2:
+            i = t // 2
+            link.send(lambda i=i: (part.at[2 * i + 1 - core], pair.at[i], ("core", i), other))
+    for i in range(NZ):
+        link.arrive(pair.at[i], ("core", i), other)
+
+    way = {1: 0, -1: 1}
+
+    def term(m, rows):
+        at = around(z, m, NZ)
+        return part[at * 2 + core, rows].astype(f32) + pair[at, rows].astype(f32)
+
+    def sum_round(k):
+        for h, rows in enumerate(cuts):
+            for d in (1, -1):
+                most = reach(d, h)
+                if k > most:
+                    continue
+                total = term(d * (most + 1 - k), rows)
+                if k > 1:
+                    link.arrive(got.at[way[d], k - 1, rows], (d, k - 1, h), other)
+                    total = total + got[way[d], k - 1, rows].astype(f32)
+                made[way[d], k, rows] = total.astype(bf16)
+                src, dst = made.at[way[d], k, rows], got.at[way[d], k, rows]
+                beside = z_device(around(z, d, NZ), core)
+                link.send(lambda s=src, t=dst, d=d, h=h, b=beside: (s, t, (d, k, h), b))
+
+    sum_round(1)
     go(hid_ring, 1)
-
-    link = Link(sum_s, sum_r)
-    order = [4, -3, 3, -2, 2, -1, 1, 0]
-    targets = {m % NZ: around(z, m, NZ) for m in order}
-    for m in order:
-        at = targets[m % NZ]
-        link.send(part.at[at * 2 + 1 - core], pair.at[at], ("core", m % NZ), other)
-    here = set()
-
-    def term(m, rows):
-        m = m % NZ
-        at = targets[m]
-        if m not in here:
-            link.arrive(pair.at[at], ("core", m), other)
-            here.add(m)
-        return part[at * 2 + core, rows].astype(f32) + pair[at, rows].astype(f32)
-
     go(hid_ring)
 
     give = []
@@ -429,34 +540,20 @@
         )
         give[e].start()
 
-    way = {1: 0, -1: 1}
-    for k in range(1, 5):
-        for h, rows in enumerate(cuts):
-            for d in (1, -1):
-                most = reach(d, h)
-                if k > most:
-                    continue
-                total = term(d * (most + 1 - k), rows)
-                if k > 1:
-                    link.arrive(got.at[way[d], k - 1, rows], (d, k - 1, h), other)
-                    total = total + got[way[d], k - 1, rows].astype(f32)
-                made[way[d], k, rows] = total.astype(bf16)
-                link.send(
-                    made.at[way[d], k, rows],
-                    got.at[way[d], k, rows],
-                    (d, k, h),
-                    z_device(around(z, d, NZ), core),
-                )
-    for e in range(EXP_DEV):
-        give[e].arrive()
-    routed = jnp.dot(one_t[...], returned[...].reshape(N_EP * 2 * ROOM, W), preferred_element_type=f32)
+    for k in range(2, 5):
+        sum_round(k)
     for h, rows in enumerate(cuts):
         total = term(0, rows)
         for d in (1, -1):
             most = reach(d, h)
             link.arrive(got.at[way[d], most, rows], (d, most, h), other)
             total = total + got[way[d], most, rows].astype(f32)
-        mixed_ref[rows, :] = total + routed[h * half : (h + 1) * half]
+        mixed_ref[rows, :] = total
+    for e in range(EXP_DEV):
+        give[e].arrive()
+    mixed_ref[...] += jnp.dot(
+        one_t[...], returned[...].reshape(N_EP * 2 * ROOM, W), preferred_element_type=f32
+    )
     for one in (ask, *dispatch, *give):
         one.finish()
     for one in (tok_link, *x_links, gu_link, dn_link, hid_link, link):
@@ -480,16 +577,23 @@
     gates,
 ):
     vmem = pl.BlockSpec(memory_space=pltpu.VMEM)
-    hbm = pl.BlockSpec(memory_space=pl.ANY)
+    hbm = pl.BlockSpec(memory_space=pltpu.HBM)
     pool = lambda *shape, dtype=bf16: pltpu.VMEM(shape, dtype)
     dma = lambda n: pltpu.SemaphoreType.DMA((n,))
     return pl.pallas_call(
         layer_kernel,
         name="layer",
         out_shape=jax.ShapeDtypeStruct((TOK_DEV, W), f32),
-        in_specs=[vmem] * 7 + [hbm] * 3,
+        in_specs=[hbm] * 10,
         out_specs=vmem,
         scratch_shapes=[
+            pool(EXP_DEV, CAP, dtype=i32),
+            pool(64, F_DEV),
+            pool(64, F_DEV),
+            pool(64, F_DEV),
+            pool(TOK_DEV, W),
+            pool(1, D, dtype=f32),
+            pool(EXP_DEV, CAP, dtype=f32),
             pool(N_EP, 1, W, dtype=i32),
             pool(64, 384),
             pool(64, 256),
@@ -503,8 +607,8 @@
             pool(N_TP, TOK_DEV, W),
             pool(EXP_DEV, CAP, W),
             pool(N_TP, EXP_DEV, CAP, W),
-            pool(N_EP, 64, 384),
-            pool(N_EP, 64, 256),
+            pool(N_EP, 2, 64, 384),
+            pool(N_EP, 2, 64, 256),
             pool(F_DEV, CAP),
             pool(N_TP, F_DEV, CAP),
             pool(EXP_DEV, N_EP, ROOM, W),
@@ -519,20 +623,21 @@
             pool(EXP_DEV, W, F),
             pool(TOK_DEV, D),
             pool(CAP, D),
-            dma(3),
+            dma(10),
             *[dma(2)] * 5,
-            *[dma(32)] * 14,
+            *[dma(64)] * 12,
+            *[dma(32)] * 2,
         ],
         compiler_params=pltpu.CompilerParams(
             collective_id=0, has_side_effects=True, vmem_limit_bytes=56 * 1024 * 1024
         ),
     )(
         chosen,
-        tokens,
-        norm_gain.reshape(1, D),
         shared_gate,
         shared_up,
         shared_down.T,
+        tokens,
+        norm_gain.reshape(1, D),
         gates,
         expert_gate.reshape(F_DEV, D),
         expert_up.reshape(F_DEV, D),

time: 97.8 us -> 92.7 us (0.948)
  Pallas kernels: 96.1 us -> 90.5 us
    pallas_call x1, Pallas kernels: 96.1 us -> 90.5 us  [on_device(): pl.pallas_call(layer_kernel, name='layer', out_shape=jax.ShapeDtypeStruct...]
where the time goes in v4:
time: 92.7 us; the launch traced here: 92.1 us
  Pallas kernels  90.5 us (98%)
  other arithmetic  1.58 us (2%)
    pallas_call x1, Pallas kernels, on_device(): pl.pallas_call(layer_kernel, name='layer', out_shape=jax.ShapeDtypeStruct...  90.5 us

profile of v4, /device:TPU:1, one launch (start us, length us, event | category | flops | bytes accessed | tf_op | source)
XLA Modules:
  0.0 92.1 jit_solution(4393797966239115275)
XLA Ops:
  0.0 90.5 %layer.1 = f32[384,128]{1,0:T(8,128)} custom-call(s32[2,384]{1,0:T(2,128)} %chosen_hbm.1, bf16[64,176]{1,0:T(8,128)(2,1)} %sg_hbm.1, bf16[64,176]{1,0:T(8,128)(2,1)} %su_hbm.1, bf16[64,176]{1,0:T(8,128)(2,1)} %bitcast.6, bf16[384,128]{1,0:T(8,128)(2,1)} %tok_hbm.1, f32[1,2048]{1,0:T(1,128)} %bitcast.7, f32[2,384]{1,0:T(2,128)} %gates_hbm.1, ...), custom_call_target="tpu_custom_call" | custom-call | tf_op jit(solution)/shard_map/layer/pallas_call | solution.py:583
  90.5 1.6 %convert_element_type.3 = bf16[384,128]{1,0:T(8,128)(2,1)} convert(f32[384,128]{1,0:T(8,128)} %layer.1) | non-fusion elementwise | flops 49152 | bytes 294912 | tf_op jit(solution)/shard_map/convert_element_type | solution.py:645

commit v5 on v4

--- a/solution.py
+++ b/solution.py
@@ -18,38 +18,55 @@
 bf16, f32, i32 = jnp.bfloat16, jnp.float32, jnp.int32
 
 
+def rows_of(ref):
+    count = ref.dtype.itemsize
+    for n in ref.shape:
+        count *= n
+    return count // (2 * W)
+
+
 class Link:
-    def __init__(self, send_sems, recv_sems):
-        self.send_sems, self.recv_sems = send_sems, recv_sems
-        self.keys, self.sent = {}, {None: [], 0: [], 1: []}
-
-    def _copy(self, src, dst, key, device):
-        i = self.keys.setdefault(key, len(self.keys))
+    def __init__(self, sems, gauge, groups):
+        self.sems, self.gauge, self.groups = sems, gauge, groups
+        self.keys, self.sent = {}, {}
+
+    def _copy(self, src, dst, key, device, group):
         return pltpu.make_async_remote_copy(
             src_ref=src,
             dst_ref=dst,
-            send_sem=self.send_sems.at[i],
-            recv_sem=self.recv_sems.at[i],
+            send_sem=self.sems.at[self.groups.index(group)],
+            recv_sem=self.sems.at[self._at(key)],
             device_id=device,
             device_id_type=MESH,
         )
 
-    def send(self, copy, core=None):
-        self._copy(*copy()).start()
-        self.sent[core].append(copy)
-
-    def arrive(self, dst, key, device):
-        self._copy(dst, dst, key, device).wait_recv()
+    def _at(self, key):
+        if key in self.groups:
+            return len(self.groups) + self.groups.index(key)
+        return 2 * len(self.groups) + self.keys.setdefault(key, len(self.keys))
+
+    def _all(self, index, rows):
+        part = self.gauge.at[pl.ds(0, rows)]
+        pltpu.make_async_copy(part, part, self.sems.at[index]).wait()
+
+    def send(self, src, dst, key, device, group, core=None):
+        self._copy(src, dst, key, device, group).start()
+        held = self.sent.setdefault((group, core), [])
+        held.append(rows_of(src))
+
+    def arrive(self, dst, key, device, group):
+        self._copy(dst, dst, key, device, group).wait_recv()
+
+    def arrive_all(self, key, rows):
+        self._all(self._at(key), rows)
 
     def finish(self):
-        for copy in self.sent[None]:
-            self._copy(*copy()).wait_send()
-        for core in (0, 1):
-
-            @on_core(core)
-            def _(core=core):
-                for copy in self.sent[core]:
-                    self._copy(*copy()).wait_send()
+        for (group, core), rows in self.sent.items():
+            at, total = self.groups.index(group), sum(rows)
+            if core is None:
+                self._all(at, total)
+            else:
+                on_core(core)(lambda at=at, total=total: self._all(at, total))
 
 
 def on_core(core):
@@ -128,32 +145,41 @@
     def mate(core):
         return z_device(place(), core)
 
+    def ring(src, at, d, k, h, c):
+        link.send(src, at, (d, k, h, c), beside(d), "ring", 1)
+
+    def hand(block):
+        link.send(block, block, "hand", mate(0), "hand", 1)
+        handed.append(rows_of(block))
+
+    handed = []
     numbered = list(enumerate(pieces))
     order = [(c, h, (flip + c) % 2, at) for c in (1, 0) for h, (flip, src, at) in numbered]
+    whole = sum(rows_of(src) for flip, src, at in pieces)
 
     @on_core(1)
     def _():
         for h, (flip, src, at) in numbered:
             for d in (1, -1):
-                link.send(lambda h=h, src=src, at=at, d=d: (src, at(place() * 2 + 1), (d, 1, h, 1), beside(d)), 1)
-        for h, (flip, src, at) in numbered:
-            link.send(lambda h=h, src=src, at=at: (src, at(place() * 2 + 1), ("core", 0, 0, h, 1), mate(0)), 1)
+                ring(src, at(place() * 2 + 1), d, 1, h, 1)
+        for flip, src, at in pieces:
+            link.send(src, at(place() * 2 + 1), "hand", mate(0), "hand", 1)
+            handed.append(rows_of(src))
 
     @on_core(0)
     def _():
-        for h, (flip, src, at) in numbered:
-            link.send(lambda h=h, src=src, at=at: (src, at(place() * 2), ("core", 0, 0, h, 0), mate(1)), 0)
+        for flip, src, at in pieces:
+            link.send(src, at(place() * 2), "join", mate(1), "join", 0)
 
     for flip, src, at in pieces:
         at(lax.axis_index("tp"))[...] = src[...]
 
     @on_core(1)
     def _():
+        link.arrive_all("join", whole)
         for h, (flip, src, at) in numbered:
-            block = lambda at=at: at(place() * 2)
-            link.arrive(block(), ("core", 0, 0, h, 0), mate(0))
             for d in (1, -1):
-                link.send(lambda h=h, b=block, d=d: (b(), b(), (d, 1, h, 0), beside(d)), 1)
+                ring(at(place() * 2), at(place() * 2), d, 1, h, 0)
 
     yield
     for k in range(1, 5):
@@ -165,23 +191,17 @@
                     most = reach(d, flip)
                     if k > most:
                         continue
-                    block = lambda at=at, d=d, c=c: at(around(place(), -d * k, NZ) * 2 + c)
-                    link.arrive(block(), (d, k, h, c), mate(0))
+                    block = at(around(place(), -d * k, NZ) * 2 + c)
+                    link.arrive(block, (d, k, h, c), mate(0), "ring")
                     if k < most:
-                        link.send(lambda b=block, d=d, h=h, c=c: (b(), b(), (d, k + 1, h, c), beside(d)), 1)
-                    link.send(lambda b=block, d=d, h=h, c=c: (b(), b(), ("core", d, k, h, c), mate(0)), 1)
+                        ring(block, block, d, k + 1, h, c)
+                    hand(block)
 
         yield
 
     @on_core(0)
     def _():
-        for h, (flip, src, at) in numbered:
-            link.arrive(at(place() * 2 + 1), ("core", 0, 0, h, 1), mate(1))
-        for k in range(1, 5):
-            for c, h, flip, at in order:
-                for d in (1, -1):
-                    if k <= reach(d, flip):
-                        link.arrive(at(around(place(), -d * k, NZ) * 2 + c), ("core", d, k, h, c), mate(1))
+        link.arrive_all("hand", sum(handed))
 
     yield
 
@@ -198,47 +218,48 @@
     def mate(core):
         return z_device(places()[0], core)
 
-    def send(key, da, db, block):
-        link.send(lambda: (block(), block(), key, {"ep": at(da, db)}), 0)
+    def ring(block, key, da, db):
+        link.send(block, block, key, {"ep": at(da, db)}, "ring", 0)
+
+    def hand(block):
+        link.send(block.at[1], block.at[1], "hand", mate(1), "hand", 0)
+        handed.append(rows_of(src))
+
+    handed = []
 
     @on_core(1)
     def _():
-        link.send(lambda: (src, dst.at[at(), 1], ("in",), mate(0)), 1)
+        link.send(src, dst.at[at(), 1], "join", mate(0), "join", 1)
 
     dst[at(), lax.rem(lax.axis_index("tp"), 2)] = src[...]
     yield
 
     @on_core(0)
     def _():
-        link.arrive(dst.at[at(), 1], ("in",), mate(1))
+        link.arrive_all("join", rows_of(src))
+        block = dst.at[at()]
         for d in (1, -1):
-            send(("a", d, 1), d, 0, lambda: dst.at[at()])
+            ring(block, ("a", d, 1), d, 0)
         for s in (1, -1):
-            send(("b", s, 1, 0), 0, s, lambda: dst.at[at()])
+            ring(block, ("b", s, 1, 0), 0, s)
 
     yield
     tags = [(0, 0)]
-    to_one = []
-
-    def share(block, key):
-        to_one.append((block, key))
-        link.send(lambda: (block().at[1], block().at[1], key, mate(1)), 0)
-
     for k in range(1, na // 2 + 1):
         for d in (1, -1):
             most = na // 2 if d > 0 else na // 2 - 1
             if k > most:
                 continue
-            block = lambda d=d, k=k: dst.at[at(-d * k, 0)]
 
             @on_core(0)
-            def _(d=d, k=k, block=block):
-                link.arrive(block(), ("a", d, k), {"ep": at()})
+            def _(d=d, k=k):
+                block = dst.at[at(-d * k, 0)]
+                link.arrive(block, ("a", d, k), {"ep": at()}, "ring")
                 if k < most:
-                    send(("a", d, k + 1), d, 0, block)
+                    ring(block, ("a", d, k + 1), d, 0)
                 for s in (1, -1):
-                    send(("b", s, 1, len(tags)), 0, s, block)
-                share(block, ("one", len(to_one)))
+                    ring(block, ("b", s, 1, len(tags)), 0, s)
+                hand(block)
 
             tags.append((d, k))
             yield
@@ -248,21 +269,20 @@
                 most = nb // 2 if (s > 0) == (n % 2 == 0) else nb // 2 - 1
                 if j > most:
                     continue
-                block = lambda d=d, k=k, s=s, j=j: dst.at[at(-d * k, -s * j)]
 
                 @on_core(0)
-                def _(s=s, j=j, n=n, block=block):
-                    link.arrive(block(), ("b", s, j, n), {"ep": at()})
+                def _(d=d, k=k, s=s, j=j, n=n):
+                    block = dst.at[at(-d * k, -s * j)]
+                    link.arrive(block, ("b", s, j, n), {"ep": at()}, "ring")
                     if j < most:
-                        send(("b", s, j + 1, n), 0, s, block)
-                    share(block, ("one", len(to_one)))
+                        ring(block, ("b", s, j + 1, n), 0, s)
+                    hand(block)
 
                 yield
 
     @on_core(1)
     def _():
-        for block, key in to_one:
-            link.arrive(block().at[1], key, mate(0))
+        link.arrive_all("hand", sum(handed))
 
     yield
 
@@ -306,7 +326,7 @@
     req_ref, gu_ref, dn_ref, wanted, asked, one_t, join, spread, out, came, tok_all, own, rows_all, wg, wd, hid, hid_all, back, returned,
     part, pair, got, made, eg, eu, ed, ed_t, normed, taken,
     load_sem, ask_sem, go_a, go_b, back_a, back_b,
-    tok_s, tok_r, xa_s, xa_r, xb_s, xb_r, gu_s, gu_r, dn_s, dn_r, hid_s, hid_r, sum_s, sum_r,
+    tok_sems, xa_sems, xb_sems, gu_sems, dn_sems, hid_sems, sum_sems,
 ):
     count = greet()
     z, core, _, _ = places()
@@ -330,16 +350,7 @@
     ]
     for load in loads:
         load.start()
-    for load in loads[:4]:
-        load.wait()
-    gu_ref[:, :W] = sg_ref[:, :W]
-    gu_ref[:, W : 2 * W] = su_ref[:, :W]
-    gu_ref[:, 2 * W :] = jnp.concatenate(
-        [sg_ref[:, W:], su_ref[:, W:], jnp.zeros((64, 32), bf16)], axis=1
-    )
-    dn_ref[...] = jnp.concatenate([sd_ref[...], jnp.zeros((64, 80), bf16)], axis=1)
-    came[...] = jnp.zeros_like(came)
-    returned[...] = jnp.zeros_like(returned)
+    loads[0].wait()
     slot_rows = []
     lane = lax.broadcasted_iota(i32, (CAP, W), 1)
     for e in range(EXP_DEV):
@@ -366,6 +377,7 @@
         both = jnp.where(side == 0, both, pltpu.roll(both, W // 2, 1))
         for j in range(NY):
             req_ref[j * NX + i] = both[j : j + 1]
+    came[...] = jnp.zeros_like(came)
     loads[4].wait()
     pl.semaphore_wait(pltpu.get_barrier_semaphore(), count)
 
@@ -382,12 +394,22 @@
         lambda p: req_ref.at[p], lambda p: asked.at[p], req_ref.at[some], asked.at[some], ask_sem
     )
     ask.start()
-    tok_link = Link(tok_s, tok_r)
+    kinds = ["ring", "hand", "join"]
+    tok_link = Link(tok_sems, rows_all, kinds)
     tok_ring = ring_gather(
-        [(h, tok_ref.at[c], lambda t, c=c: tok_all.at[t, c]) for h, c in enumerate(cuts)], tok_link
+        [(0, tok_ref, lambda t: tok_all.at[t])], tok_link
     )
     go(tok_ring, 1)
-    gu_link, dn_link = Link(gu_s, gu_r), Link(dn_s, dn_r)
+    for load in loads[1:4]:
+        load.wait()
+    returned[...] = jnp.zeros_like(returned)
+    gu_ref[:, :W] = sg_ref[:, :W]
+    gu_ref[:, W : 2 * W] = su_ref[:, :W]
+    gu_ref[:, 2 * W :] = jnp.concatenate(
+        [sg_ref[:, W:], su_ref[:, W:], jnp.zeros((64, 32), bf16)], axis=1
+    )
+    dn_ref[...] = jnp.concatenate([sd_ref[...], jnp.zeros((64, 80), bf16)], axis=1)
+    gu_link, dn_link = Link(gu_sems, rows_all, kinds), Link(dn_sems, rows_all, kinds)
     gu_job = plane_gather(gu_ref, wg, gu_link, True)
     dn_job = plane_gather(dn_ref, wd, dn_link, False)
     go(gu_job, 1)
@@ -427,8 +449,12 @@
     go(tok_ring, 1)
     go(tok_ring, 1)
 
-    x_links = [Link(xa_s, xa_r), Link(xb_s, xb_r)]
+    x_links = [Link(xa_sems, rows_all, kinds), Link(xb_sems, rows_all, kinds)]
     x_rings = []
+
+    def taken_rows(t, e):
+        return pl.ds(pl.multiple_of((t * EXP_DEV + e) * CAP, CAP), CAP)
+
     for e in range(EXP_DEV):
         dispatch[e].arrive()
         own[e] = jnp.dot(
@@ -436,10 +462,7 @@
         ).astype(bf16)
         x_rings.append(
             ring_gather(
-                [
-                    (e + h, own.at[e, c], lambda t, c=c, e=e: rows_all.at[t, e, c])
-                    for h, c in enumerate(cuts)
-                ],
+                [(e, own.at[e], lambda t, e=e: rows_all.at[taken_rows(t, e)])],
                 x_links[e],
             )
         )
@@ -456,11 +479,11 @@
         go(x_rings[e], 1)
 
     expert = z // (NZ // EXP_DEV)
-    normalise(lambda t: rows_all.at[t, expert], gain_ref, taken)
+    normalise(lambda t: rows_all.at[taken_rows(t, expert)], gain_ref, taken)
     gate_values = lax.dot_general(eg[...], taken[...], dims(1, 1), preferred_element_type=f32)
     up_values = lax.dot_general(eu[...], taken[...], dims(1, 1), preferred_element_type=f32)
     hid[...] = (silu(gate_values) * up_values).astype(bf16)
-    hid_link = Link(hid_s, hid_r)
+    hid_link = Link(hid_sems, rows_all, kinds)
     hid_ring = ring_gather(
         [
             (h, hid.at[c], lambda t, c=c: hid_all.at[t, c])
@@ -486,16 +509,15 @@
     shared = jnp.concatenate([low, high, jnp.zeros((TOK_DEV, 80), f32)], axis=1).astype(bf16)
     go(hid_ring, 1)
     go(dn_job)
-    link = Link(sum_s, sum_r)
+    link = Link(sum_sems, rows_all, ["pair", "ring"])
     for t in range(N_TP):
         weights = wd[2 * t : 2 * t + 2, mine].reshape(W, 256)
         block = lax.dot_general(shared, weights, dims(1, 1), preferred_element_type=f32)
         part[t] = block.astype(bf16)
         if t % 2:
             i = t // 2
-            link.send(lambda i=i: (part.at[2 * i + 1 - core], pair.at[i], ("core", i), other))
-    for i in range(NZ):
-        link.arrive(pair.at[i], ("core", i), other)
+            link.send(part.at[2 * i + 1 - core], pair.at[i], "pair", other, "pair")
+    link.arrive_all("pair", NZ * TOK_DEV)
 
     way = {1: 0, -1: 1}
 
@@ -511,12 +533,12 @@
                     continue
                 total = term(d * (most + 1 - k), rows)
                 if k > 1:
-                    link.arrive(got.at[way[d], k - 1, rows], (d, k - 1, h), other)
+                    link.arrive(got.at[way[d], k - 1, rows], (d, k - 1, h), other, "ring")
                     total = total + got[way[d], k - 1, rows].astype(f32)
                 made[way[d], k, rows] = total.astype(bf16)
                 src, dst = made.at[way[d], k, rows], got.at[way[d], k, rows]
                 beside = z_device(around(z, d, NZ), core)
-                link.send(lambda s=src, t=dst, d=d, h=h, b=beside: (s, t, (d, k, h), b))
+                link.send(src, dst, (d, k, h), beside, "ring")
 
     sum_round(1)
     go(hid_ring, 1)
@@ -546,7 +568,7 @@
         total = term(0, rows)
         for d in (1, -1):
             most = reach(d, h)
-            link.arrive(got.at[way[d], most, rows], (d, most, h), other)
+            link.arrive(got.at[way[d], most, rows], (d, most, h), other, "ring")
             total = total + got[way[d], most, rows].astype(f32)
         mixed_ref[rows, :] = total
     for e in range(EXP_DEV):
@@ -606,7 +628,7 @@
             pool(EXP_DEV, N_EP, ROOM, W),
             pool(N_TP, TOK_DEV, W),
             pool(EXP_DEV, CAP, W),
-            pool(N_TP, EXP_DEV, CAP, W),
+            pool(N_TP * EXP_DEV * CAP, W),
             pool(N_EP, 2, 64, 384),
             pool(N_EP, 2, 64, 256),
             pool(F_DEV, CAP),
@@ -625,8 +647,10 @@
             pool(CAP, D),
             dma(10),
             *[dma(2)] * 5,
-            *[dma(64)] * 12,
-            *[dma(32)] * 2,
+            *[dma(20)] * 3,
+            *[dma(37)] * 2,
+            dma(34),
+            dma(18),
         ],
         compiler_params=pltpu.CompilerParams(
             collective_id=0, has_side_effects=True, vmem_limit_bytes=56 * 1024 * 1024

time: 92.7 us -> 87.4 us (0.943)
  Pallas kernels: 90.5 us -> 84.5 us
    pallas_call x1, Pallas kernels: 90.5 us -> 84.5 us  [on_device(): pl.pallas_call(layer_kernel, name='layer', out_shape=jax.ShapeDtypeStruct...]
where the time goes in v5:
time: 87.4 us; the launch traced here: 86 us
  Pallas kernels  84.5 us (97%)
  other arithmetic  1.58 us (2%)
    pallas_call x1, Pallas kernels, on_device(): pl.pallas_call(layer_kernel, name='layer', out_shape=jax.ShapeDtypeStruct...  84.5 us

profile of v5, /device:TPU:1, one launch (start us, length us, event | category | flops | bytes accessed | tf_op | source)
XLA Modules:
  0.0 86.0 jit_solution(16606535414719654771)
XLA Ops:
  0.0 84.5 %layer.1 = f32[384,128]{1,0:T(8,128)} custom-call(s32[2,384]{1,0:T(2,128)} %chosen_hbm.1, bf16[64,176]{1,0:T(8,128)(2,1)} %sg_hbm.1, bf16[64,176]{1,0:T(8,128)(2,1)} %su_hbm.1, bf16[64,176]{1,0:T(8,128)(2,1)} %bitcast.6, bf16[384,128]{1,0:T(8,128)(2,1)} %tok_hbm.1, f32[1,2048]{1,0:T(1,128)} %bitcast.7, f32[2,384]{1,0:T(2,128)} %gates_hbm.1, ...), custom_call_target="tpu_custom_call" | custom-call | tf_op jit(solution)/shard_map/layer/pallas_call | solution.py:605
  84.5 1.6 %convert_element_type.3 = bf16[384,128]{1,0:T(8,128)(2,1)} convert(f32[384,128]{1,0:T(8,128)} %layer.1) | non-fusion elementwise | flops 49152 | bytes 294912 | tf_op jit(solution)/shard_map/convert_element_type | solution.py:669

commit v6 on v5

--- a/solution.py
+++ b/solution.py
@@ -184,9 +184,10 @@
     yield
     for k in range(1, 5):
 
-        @on_core(1)
-        def _(k=k):
-            for c, h, flip, at in order:
+        for c, h, flip, at in order:
+
+            @on_core(1)
+            def _(k=k, c=c, h=h, flip=flip, at=at):
                 for d in (1, -1):
                     most = reach(d, flip)
                     if k > most:
@@ -197,7 +198,7 @@
                         ring(block, block, d, k + 1, h, c)
                     hand(block)
 
-        yield
+            yield
 
     @on_core(0)
     def _():
@@ -244,41 +245,35 @@
             ring(block, ("b", s, 1, 0), 0, s)
 
     yield
-    tags = [(0, 0)]
-    for k in range(1, na // 2 + 1):
-        for d in (1, -1):
-            most = na // 2 if d > 0 else na // 2 - 1
-            if k > most:
-                continue
-
-            @on_core(0)
-            def _(d=d, k=k):
-                block = dst.at[at(-d * k, 0)]
-                link.arrive(block, ("a", d, k), {"ep": at()}, "ring")
-                if k < most:
-                    ring(block, ("a", d, k + 1), d, 0)
+    def most(d, n, length):
+        return length // 2 if (d > 0) == (n % 2 == 0) else length // 2 - 1
+
+    tags = [(0, 0)] + [(d, k) for k in range(1, na // 2 + 1) for d in (1, -1) if k <= most(d, 0, na)]
+    for wave in range(1, na // 2 + nb // 2 + 1):
+
+        @on_core(0)
+        def _(wave=wave):
+            for n, (d, k) in enumerate(tags):
+                if k == wave:
+                    block = dst.at[at(-d * k, 0)]
+                    link.arrive(block, ("a", d, k), {"ep": at()}, "ring")
+                    if k < most(d, 0, na):
+                        ring(block, ("a", d, k + 1), d, 0)
+                    for s in (1, -1):
+                        ring(block, ("b", s, 1, n), 0, s)
+                    hand(block)
+            for n, (d, k) in enumerate(tags):
+                j = wave - k
                 for s in (1, -1):
-                    ring(block, ("b", s, 1, len(tags)), 0, s)
-                hand(block)
-
-            tags.append((d, k))
-            yield
-    for j in range(1, nb // 2 + 1):
-        for n, (d, k) in enumerate(tags):
-            for s in (1, -1):
-                most = nb // 2 if (s > 0) == (n % 2 == 0) else nb // 2 - 1
-                if j > most:
-                    continue
-
-                @on_core(0)
-                def _(d=d, k=k, s=s, j=j, n=n):
+                    if not 1 <= j <= most(s, n, nb):
+                        continue
                     block = dst.at[at(-d * k, -s * j)]
                     link.arrive(block, ("b", s, j, n), {"ep": at()}, "ring")
-                    if j < most:
+                    if j < most(s, n, nb):
                         ring(block, ("b", s, j + 1, n), 0, s)
                     hand(block)
 
-                yield
+        yield
 
     @on_core(1)
     def _():
@@ -324,11 +319,10 @@
     mixed_ref,
     chosen_ref, sg_ref, su_ref, sd_ref, tok_ref, gain_ref, gates_ref,
     req_ref, gu_ref, dn_ref, wanted, asked, one_t, join, spread, out, came, tok_all, own, rows_all, wg, wd, hid, hid_all, back, returned,
-    part, pair, got, made, eg, eu, ed, ed_t, normed, taken,
+    part, pair, got, made, eg, eu, ed, ed_t, normed, taken, shared,
     load_sem, ask_sem, go_a, go_b, back_a, back_b,
-    tok_sems, xa_sems, xb_sems, gu_sems, dn_sems, hid_sems, sum_sems,
+    turn_sem, tok_sems, xa_sems, xb_sems, gu_sems, dn_sems, hid_sems, sum_sems,
 ):
-    count = greet()
     z, core, _, _ = places()
     other = z_device(z, 1 - core)
     loads = [
@@ -350,6 +344,7 @@
     ]
     for load in loads:
         load.start()
+    count = greet()
     loads[0].wait()
     slot_rows = []
     lane = lax.broadcasted_iota(i32, (CAP, W), 1)
@@ -417,7 +412,9 @@
     for e in range(EXP_DEV):
         at = lax.broadcasted_iota(i32, (N_EP * ROOM, CAP), 0)
         spread[e] = one_hot(at == slot_rows[e])
-    go(tok_ring, 1)
+    go(gu_job, 1)
+    go(dn_job, 1)
+    go(tok_ring, 2)
 
     ask.arrive()
     token = lax.broadcasted_iota(i32, (TOK_DEV, W), 0)
@@ -446,8 +443,8 @@
         load.wait()
     for e in range(EXP_DEV):
         ed_t[e] = ed[e].T
-    go(tok_ring, 1)
-    go(tok_ring, 1)
+    go(tok_ring, 2)
+    go(tok_ring, 2)
 
     x_links = [Link(xa_sems, rows_all, kinds), Link(xb_sems, rows_all, kinds)]
     x_rings = []
@@ -468,13 +465,13 @@
         )
         go(x_rings[e], 1)
         if e == 0:
-            go(tok_ring, 1)
-    for k in range(13):
+            go(tok_ring, 2)
+    for wave in range(4):
         go(gu_job, 1)
         go(dn_job, 1)
     for k in range(4):
         for e in range(EXP_DEV):
-            go(x_rings[e], 1)
+            go(x_rings[e], 2)
     for e in range(EXP_DEV):
         go(x_rings[e], 1)
 
@@ -493,26 +490,30 @@
     )
     go(hid_ring, 1)
 
-    for k in range(18):
+    go(tok_ring)
+    normalise(lambda t: tok_all.at[t], gain_ref, normed)
+    for wave in range(2):
         go(gu_job, 1)
         go(dn_job, 1)
-    go(tok_ring)
-    normalise(lambda t: tok_all.at[t], gain_ref, normed)
+    go(hid_ring, 4)
+    go(gu_job)
     go(hid_ring, 1)
-    go(hid_ring, 1)
-    go(gu_job)
     mine = pl.ds(core, 1)
     weights = wg[:, mine].reshape(D, 384)
-    sums = jnp.dot(normed[...], weights, preferred_element_type=f32)
-    low = silu(sums[:, :W]) * sums[:, W : 2 * W]
-    high = silu(sums[:, 256:304]) * sums[:, 304:352]
-    shared = jnp.concatenate([low, high, jnp.zeros((TOK_DEV, 80), f32)], axis=1).astype(bf16)
-    go(hid_ring, 1)
+    for i in range(3):
+        block = pl.ds(i * W, W)
+        sums = jnp.dot(normed[block, :], weights, preferred_element_type=f32)
+        low = silu(sums[:, :W]) * sums[:, W : 2 * W]
+        high = silu(sums[:, 256:304]) * sums[:, 304:352]
+        shared[block, :] = jnp.concatenate([low, high, jnp.zeros((W, 80), f32)], axis=1).astype(bf16)
+        go(hid_ring, 1)
     go(dn_job)
     link = Link(sum_sems, rows_all, ["pair", "ring"])
     for t in range(N_TP):
+        if t % 4 == 0:
+            go(hid_ring, 1)
         weights = wd[2 * t : 2 * t + 2, mine].reshape(W, 256)
-        block = lax.dot_general(shared, weights, dims(1, 1), preferred_element_type=f32)
+        block = lax.dot_general(shared[...], weights, dims(1, 1), preferred_element_type=f32)
         part[t] = block.astype(bf16)
         if t % 2:
             i = t // 2
@@ -540,8 +541,17 @@
                 beside = z_device(around(z, d, NZ), core)
                 link.send(src, dst, (d, k, h), beside, "ring")
 
+
+    @on_core(1)
+    def _():
+        pl.semaphore_signal(turn_sem, inc=1, device_id=other, device_id_type=MESH)
+
+    @on_core(0)
+    def _():
+        pl.semaphore_wait(turn_sem, 1)
+
     sum_round(1)
-    go(hid_ring, 1)
+    go(hid_ring, 4)
     go(hid_ring)
 
     give = []
@@ -561,8 +571,10 @@
             )
         )
         give[e].start()
-
-    for k in range(2, 5):
+        if e == 0:
+            sum_round(2)
+
+    for k in range(3, 5):
         sum_round(k)
     for h, rows in enumerate(cuts):
         total = term(0, rows)
@@ -645,8 +657,10 @@
             pool(EXP_DEV, W, F),
             pool(TOK_DEV, D),
             pool(CAP, D),
+            pool(TOK_DEV, 256),
             dma(10),
             *[dma(2)] * 5,
+            pltpu.SemaphoreType.REGULAR,
             *[dma(20)] * 3,
             *[dma(37)] * 2,
             dma(34),

time: 87.4 us -> 85.9 us (0.983)
  the two profiles are of different devices: /device:TPU:1 before, /device:TPU:2 now
where the time goes in v6:
time: 85.9 us; the launch traced here: 85.8 us
  Pallas kernels  84.2 us (98%)
  other arithmetic  1.58 us (2%)
    pallas_call x1, Pallas kernels, on_device(): pl.pallas_call(layer_kernel, name='layer', out_shape=jax.ShapeDtypeStruct...  84.2 us

profile of v6, /device:TPU:2, one launch (start us, length us, event | category | flops | bytes accessed | tf_op | source)
XLA Modules:
  0.0 85.8 jit_solution(17068581053309718986)
XLA Ops:
  0.0 84.2 %layer.1 = f32[384,128]{1,0:T(8,128)} custom-call(s32[2,384]{1,0:T(2,128)} %chosen_hbm.1, bf16[64,176]{1,0:T(8,128)(2,1)} %sg_hbm.1, bf16[64,176]{1,0:T(8,128)(2,1)} %su_hbm.1, bf16[64,176]{1,0:T(8,128)(2,1)} %bitcast.6, bf16[384,128]{1,0:T(8,128)(2,1)} %tok_hbm.1, f32[1,2048]{1,0:T(1,128)} %bitcast.7, f32[2,384]{1,0:T(2,128)} %gates_hbm.1, ...), custom_call_target="tpu_custom_call" | custom-call | tf_op jit(solution)/shard_map/layer/pallas_call | solution.py:617
  84.2 1.6 %convert_element_type.3 = bf16[384,128]{1,0:T(8,128)(2,1)} convert(f32[384,128]{1,0:T(8,128)} %layer.1) | non-fusion elementwise | flops 49152 | bytes 294912 | tf_op jit(solution)/shard_map/convert_element_type | solution.py:683

commit v7 on v6

--- a/solution.py
+++ b/solution.py
@@ -31,10 +31,11 @@
         self.keys, self.sent = {}, {}
 
     def _copy(self, src, dst, key, device, group):
+        sent = self.groups.index(group) if group in self.groups else self._at(("sent", key))
         return pltpu.make_async_remote_copy(
             src_ref=src,
             dst_ref=dst,
-            send_sem=self.sems.at[self.groups.index(group)],
+            send_sem=self.sems.at[sent],
             recv_sem=self.sems.at[self._at(key)],
             device_id=device,
             device_id_type=MESH,
@@ -49,10 +50,10 @@
         part = self.gauge.at[pl.ds(0, rows)]
         pltpu.make_async_copy(part, part, self.sems.at[index]).wait()
 
-    def send(self, src, dst, key, device, group, core=None):
+    def send(self, src, dst, key, device, group, core=None, wanted=None):
         self._copy(src, dst, key, device, group).start()
-        held = self.sent.setdefault((group, core), [])
-        held.append(rows_of(src))
+        at = self.groups.index(group) if group in self.groups else self._at(("sent", key))
+        self.sent.setdefault((at, core), [wanted, 0])[1] += rows_of(src)
 
     def arrive(self, dst, key, device, group):
         self._copy(dst, dst, key, device, group).wait_recv()
@@ -61,12 +62,15 @@
         self._all(self._at(key), rows)
 
     def finish(self):
-        for (group, core), rows in self.sent.items():
-            at, total = self.groups.index(group), sum(rows)
-            if core is None:
-                self._all(at, total)
-            else:
-                on_core(core)(lambda at=at, total=total: self._all(at, total))
+        for (at, core), (wanted, rows) in self.sent.items():
+            here = True if core is None else lax.rem(lax.axis_index("tp"), 2) == core
+            if wanted is not None:
+                here = jnp.logical_and(here, wanted())
+            when(here)(lambda at=at, rows=rows: self._all(at, rows))
+
+
+def when(condition):
+    return (lambda f: f()) if condition is True else pl.when(condition)
 
 
 def on_core(core):
@@ -135,7 +139,7 @@
     return 4 if (direction > 0) != bool(flipped) else 3
 
 
-def ring_gather(pieces, link):
+def ring_gather(pieces, link, taker=None):
     def place():
         return lax.axis_index("tp") // 2
 
@@ -145,12 +149,27 @@
     def mate(core):
         return z_device(place(), core)
 
-    def ring(src, at, d, k, h, c):
-        link.send(src, at, (d, k, h, c), beside(d), "ring", 1)
-
-    def hand(block):
-        link.send(block, block, "hand", mate(0), "hand", 1)
-        handed.append(rows_of(block))
+    def takes():
+        return True if taker is None else place() // (NZ // EXP_DEV) == taker
+
+    def goes(d, k, flip, back):
+        if taker is None:
+            return True
+        half = NZ // EXP_DEV
+        v = lax.rem(place() - d * back - half * taker + 2 * NZ, NZ)
+        if d < 0:
+            v = lax.rem(half - 1 - v + NZ, NZ)
+        last = half - 1 if reach(d, flip) == half else half
+        return jnp.logical_or(v < half - k, v > last)
+
+    def ring(src, at, d, k, h, c, flip, back):
+        key, group = (d, k, h, c), "ring" if taker is None else None
+        wanted = None if taker is None else lambda: goes(d, k, flip, back)
+        link.send(src, at, key, beside(d), group, 1, wanted)
+
+    def hand(src, dst):
+        link.send(src, dst, "hand", mate(0), "hand", 1, None if taker is None else takes)
+        handed.append(rows_of(src))
 
     handed = []
     numbered = list(enumerate(pieces))
@@ -161,10 +180,13 @@
     def _():
         for h, (flip, src, at) in numbered:
             for d in (1, -1):
-                ring(src, at(place() * 2 + 1), d, 1, h, 1)
+
+                @when(goes(d, 1, (flip + 1) % 2, 0))
+                def _(d=d, h=h, flip=flip, src=src, at=at):
+                    ring(src, at(place() * 2 + 1), d, 1, h, 1, (flip + 1) % 2, 0)
+
         for flip, src, at in pieces:
-            link.send(src, at(place() * 2 + 1), "hand", mate(0), "hand", 1)
-            handed.append(rows_of(src))
+            when(takes())(lambda src=src, at=at: hand(src, at(place() * 2 + 1)))
 
     @on_core(0)
     def _():
@@ -179,30 +201,33 @@
         link.arrive_all("join", whole)
         for h, (flip, src, at) in numbered:
             for d in (1, -1):
-                ring(at(place() * 2), at(place() * 2), d, 1, h, 0)
+
+                @when(goes(d, 1, flip, 0))
+                def _(d=d, h=h, flip=flip, at=at):
+                    ring(at(place() * 2), at(place() * 2), d, 1, h, 0, flip, 0)
 
     yield
     for k in range(1, 5):
-
         for c, h, flip, at in order:
 
+            def step(d, k=k, c=c, h=h, flip=flip, at=at):
+                block = at(around(place(), -d * k, NZ) * 2 + c)
+                link.arrive(block, (d, k, h, c), mate(0), "ring" if taker is None else None)
+                if k < reach(d, flip):
+                    when(goes(d, k + 1, flip, k))(lambda: ring(block, block, d, k + 1, h, c, flip, k))
+                when(takes())(lambda: hand(block, block))
+
             @on_core(1)
-            def _(k=k, c=c, h=h, flip=flip, at=at):
+            def _(k=k, flip=flip, step=step):
                 for d in (1, -1):
-                    most = reach(d, flip)
-                    if k > most:
-                        continue
-                    block = at(around(place(), -d * k, NZ) * 2 + c)
-                    link.arrive(block, (d, k, h, c), mate(0), "ring")
-                    if k < most:
-                        ring(block, block, d, k + 1, h, c)
-                    hand(block)
+                    if k <= reach(d, flip):
+                        when(goes(d, k, flip, k))(lambda d=d: step(d))
 
             yield
 
     @on_core(0)
     def _():
-        link.arrive_all("hand", sum(handed))
+        when(takes())(lambda: link.arrive_all("hand", sum(handed)))
 
     yield
 
@@ -461,12 +486,15 @@
             ring_gather(
                 [(e, own.at[e], lambda t, e=e: rows_all.at[taken_rows(t, e)])],
                 x_links[e],
+                e,
             )
         )
         go(x_rings[e], 1)
         if e == 0:
             go(tok_ring, 2)
-    for wave in range(4):
+            go(gu_job, 1)
+            go(dn_job, 1)
+    for wave in range(3):
         go(gu_job, 1)
         go(dn_job, 1)
     for k in range(4):
@@ -571,10 +599,8 @@
             )
         )
         give[e].start()
-        if e == 0:
-            sum_round(2)
-
-    for k in range(3, 5):
+
+    for k in range(2, 5):
         sum_round(k)
     for h, rows in enumerate(cuts):
         total = term(0, rows)
@@ -661,7 +687,8 @@
             dma(10),
             *[dma(2)] * 5,
             pltpu.SemaphoreType.REGULAR,
-            *[dma(20)] * 3,
+            dma(20),
+            *[dma(34)] * 2,
             *[dma(37)] * 2,
             dma(34),
             dma(18),

time: 85.9 us -> 83.2 us (0.969)
  the two profiles are of different devices: /device:TPU:2 before, /device:TPU:1 now
where the time goes in v7:
time: 83.2 us; the launch traced here: 82.4 us
  Pallas kernels  80.8 us (97%)
  other arithmetic  1.58 us (2%)
    pallas_call x1, Pallas kernels, on_device(): pl.pallas_call(layer_kernel, name='layer', out_shape=jax.ShapeDtypeStruct...  80.8 us

profile of v7, /device:TPU:1, one launch (start us, length us, event | category | flops | bytes accessed | tf_op | source)
XLA Modules:
  0.0 82.4 jit_solution(6676691546259026140)
XLA Ops:
  0.0 80.8 %layer.1 = f32[384,128]{1,0:T(8,128)} custom-call(s32[2,384]{1,0:T(2,128)} %chosen_hbm.1, bf16[64,176]{1,0:T(8,128)(2,1)} %sg_hbm.1, bf16[64,176]{1,0:T(8,128)(2,1)} %su_hbm.1, bf16[64,176]{1,0:T(8,128)(2,1)} %bitcast.6, bf16[384,128]{1,0:T(8,128)(2,1)} %tok_hbm.1, f32[1,2048]{1,0:T(1,128)} %bitcast.7, f32[2,384]{1,0:T(2,128)} %gates_hbm.1, ...), custom_call_target="tpu_custom_call" | custom-call | tf_op jit(solution)/shard_map/layer/pallas_call | solution.py:643
  80.9 1.6 %convert_element_type.3 = bf16[384,128]{1,0:T(8,128)(2,1)} convert(f32[384,128]{1,0:T(8,128)} %layer.1) | non-fusion elementwise | flops 49152 | bytes 294912 | tf_op jit(solution)/shard_map/convert_element_type | solution.py:710

commit v8 on v7

--- a/solution.py
+++ b/solution.py
@@ -92,7 +92,7 @@
 
 OFFSETS = sorted(
     [(a, b) for a in range(-3, 5) for b in range(-1, 3) if (a, b) != (0, 0)],
-    key=lambda o: (o[1] % 4, o[0] % 8),
+    key=lambda o: (o[1] % 4, -abs(o[0]), o[0]),
 )
 
 
@@ -344,7 +344,7 @@
     mixed_ref,
     chosen_ref, sg_ref, su_ref, sd_ref, tok_ref, gain_ref, gates_ref,
     req_ref, gu_ref, dn_ref, wanted, asked, one_t, join, spread, out, came, tok_all, own, rows_all, wg, wd, hid, hid_all, back, returned,
-    part, pair, got, made, eg, eu, ed, ed_t, normed, taken, shared,
+    part, pair, got, made, eg, eu, ed, ed_t, normed, taken, shared, slot_columns,
     load_sem, ask_sem, go_a, go_b, back_a, back_b,
     turn_sem, tok_sems, xa_sems, xb_sems, gu_sems, dn_sems, hid_sems, sum_sems,
 ):
@@ -384,10 +384,10 @@
         slots = sources * ROOM + lax.broadcasted_iota(i32, (1, CAP), 1) - before
         slot_rows.append(slots)
         slots_down = jnp.broadcast_to(slots, (W, CAP)).T
+        slot_columns[e] = slots_down
         local = ids_down - sources_down * TOK_DEV
         for b in range(N_EP * ROOM // W):
             match = slots_down == lane + b * W
-            join[e, :, b * W : (b + 1) * W] = one_hot(match)
             wanted[e, b : b + 1] = jnp.max(jnp.where(match, local, -1), axis=0, keepdims=True)
     side = lax.rem(lax.axis_index("ep"), 2)
     lane = lax.broadcasted_iota(i32, (NY, W), 1)
@@ -437,6 +437,9 @@
     for e in range(EXP_DEV):
         at = lax.broadcasted_iota(i32, (N_EP * ROOM, CAP), 0)
         spread[e] = one_hot(at == slot_rows[e])
+        lane = lax.broadcasted_iota(i32, (CAP, W), 1)
+        for b in range(N_EP * ROOM // W):
+            join[e, :, b * W : (b + 1) * W] = one_hot(slot_columns[e] == lane + b * W)
     go(gu_job, 1)
     go(dn_job, 1)
     go(tok_ring, 2)
@@ -684,6 +687,7 @@
             pool(TOK_DEV, D),
             pool(CAP, D),
             pool(TOK_DEV, 256),
+            pool(EXP_DEV, CAP, W, dtype=i32),
             dma(10),
             *[dma(2)] * 5,
             pltpu.SemaphoreType.REGULAR,

time: 83.2 us -> 83 us (level)
  no operation moved by 1% of the time
where the time goes in v8:
time: 83 us; the launch traced here: 81.8 us
  Pallas kernels  80.2 us (97%)
  other arithmetic  1.58 us (2%)
    pallas_call x1, Pallas kernels, on_device(): pl.pallas_call(layer_kernel, name='layer', out_shape=jax.ShapeDtypeStruct...  80.2 us

profile of v8, /device:TPU:1, one launch (start us, length us, event | category | flops | bytes accessed | tf_op | source)
XLA Modules:
  0.0 81.8 jit_solution(15598694570253959662)
XLA Ops:
  0.0 80.2 %layer.1 = f32[384,128]{1,0:T(8,128)} custom-call(s32[2,384]{1,0:T(2,128)} %chosen_hbm.1, bf16[64,176]{1,0:T(8,128)(2,1)} %sg_hbm.1, bf16[64,176]{1,0:T(8,128)(2,1)} %su_hbm.1, bf16[64,176]{1,0:T(8,128)(2,1)} %bitcast.6, bf16[384,128]{1,0:T(8,128)(2,1)} %tok_hbm.1, f32[1,2048]{1,0:T(1,128)} %bitcast.7, f32[2,384]{1,0:T(2,128)} %gates_hbm.1, ...), custom_call_target="tpu_custom_call" | custom-call | tf_op jit(solution)/shard_map/layer/pallas_call | solution.py:646
  80.2 1.6 %convert_element_type.3 = bf16[384,128]{1,0:T(8,128)(2,1)} convert(f32[384,128]{1,0:T(8,128)} %layer.1) | non-fusion elementwise | flops 49152 | bytes 294912 | tf_op jit(solution)/shard_map/convert_element_type | solution.py:714
